TPU v7x, 8 devices: a whole 2x2x1 slice. The times are simulated.
8 devices in a mesh: dp: 1 (over z), tp: 2 (over y), pp: 4 (over x, core).
Axes of the slice: x: 2, y: 2, z: 1, core: 2. Of those that a mesh axis runs over, the one named last changes fastest.
Arguments:
- tokens: int32 [4, 64], P('dp')
- labels: int32 [4, 64], P('dp')
- emb_table: bfloat16 [50272, 2048], P('tp')
- w_in: bfloat16 [4, 2048, 8192], P('pp', None, 'tp')
- w_out: bfloat16 [4, 8192, 2048], P('pp', 'tp')
Outputs:
- output 1: float32 [1], P('dp')
- output 2: float32 [4, 2048, 8192], P(('dp', 'pp'), None, 'tp')
- output 3: float32 [4, 8192, 2048], P(('dp', 'pp'), 'tp')
- output 4: float32 [50272, 2048], P(('dp', 'tp'))
All inputs are finite; a program needn't handle non-finite values.
Results may differ from a plain program's by a relative error of at most 0.0108034.
Values are sent between devices in bfloat16 or wider.
A program may use at most 1.75 GiB of HBM per device.

v0:
```python
import jax
import jax.numpy as jnp
from jax import lax
from jax.sharding import PartitionSpec as P

NORM_EPS = 1e-6


def contract(lhs, rhs, lhs_dim, rhs_dim):
    return lax.dot_general(lhs, rhs, (((lhs_dim,), (rhs_dim,)), ((), ())), preferred_element_type=jnp.float32)


def solution(mesh):
    pp_size = mesh.shape['pp']
    fwd_perm = [(src_stage, src_stage + 1) for src_stage in range(pp_size - 1)]
    bwd_perm = [(src_stage + 1, src_stage) for src_stage in range(pp_size - 1)]

    def device_fn(tokens, labels, emb_table, w_in, w_out):
        num_micro, seq_len = tokens.shape
        vocab_rows, model_dim = emb_table.shape
        w_one = w_in[0]
        w_two = w_out[0]
        hidden_cols = w_one.shape[1]
        stage_idx = lax.axis_index('pp')
        is_first = stage_idx == 0
        is_last = stage_idx == pp_size - 1
        vocab_base = lax.axis_index('tp') * vocab_rows
        tok_local = tokens - vocab_base
        lab_local = labels - vocab_base
        row_ids = jnp.arange(vocab_rows, dtype=jnp.int32)
        num_ticks = num_micro + pp_size - 1
        act_zero = jnp.zeros((seq_len, model_dim), jnp.bfloat16)

        owned_ids = (tok_local >= 0) & (tok_local < vocab_rows) & is_first
        looked_up = jnp.take(emb_table, jnp.clip(tok_local, 0, vocab_rows - 1), axis=0)
        x_first = lax.psum(jnp.where(owned_ids[:, :, None], looked_up, jnp.zeros_like(looked_up)), 'tp')

        def fwd_tick(x_recv, tick_idx):
            fresh_in = lax.dynamic_index_in_dim(x_first, jnp.minimum(tick_idx, num_micro - 1), 0, keepdims=False)
            x_act = jnp.where(is_first, fresh_in, x_recv)
            hidden = jnp.dot(x_act, w_one, preferred_element_type=jnp.float32)
            gate_act = jax.nn.gelu(hidden).astype(jnp.bfloat16)
            branch_out = lax.psum(jnp.dot(gate_act, w_two, preferred_element_type=jnp.float32), 'tp')
            y_act = (x_act.astype(jnp.float32) + branch_out).astype(jnp.bfloat16)
            return lax.ppermute(y_act, 'pp', fwd_perm), (x_act, hidden, y_act)

        x_hist, h_hist, y_hist = lax.scan(fwd_tick, act_zero, jnp.arange(num_ticks))[1]
        x_saved = lax.dynamic_slice_in_dim(x_hist, stage_idx, num_micro, 0)
        h_saved = lax.dynamic_slice_in_dim(h_hist, stage_idx, num_micro, 0)
        y_top = y_hist[pp_size - 1:]

        def head_step(carry_in, micro_in):
            loss_sum, head_grad = carry_in
            y_act, lab_row = micro_in
            x_wide = y_act.astype(jnp.float32)
            inv_rms = lax.rsqrt(jnp.mean(x_wide * x_wide, axis=-1, keepdims=True) + NORM_EPS)
            normed = x_wide * inv_rms
            normed_b = normed.astype(jnp.bfloat16)
            target_hit = lab_row[:, None] == row_ids[None, :]

            def logit_part():
                logits = contract(normed_b, emb_table, 1, 1)
                local_lse = jax.nn.logsumexp(logits, axis=-1)
                local_target = jnp.sum(jnp.where(target_hit, logits, 0.0), axis=-1)
                return logits, local_lse, local_target

            def logit_skip():
                flat_zero = jnp.zeros((seq_len,), jnp.float32)
                return jnp.zeros((seq_len, vocab_rows), jnp.float32), flat_zero, flat_zero

            logits, local_lse, local_target = lax.cond(is_last, logit_part, logit_skip)
            log_norm = jax.nn.logsumexp(lax.all_gather(local_lse, 'tp'), axis=0)
            target_logit = lax.psum(local_target, 'tp')

            def grad_part():
                grad_logits = (jnp.exp(logits - log_norm[:, None]) - target_hit.astype(jnp.float32)).astype(jnp.bfloat16)
                return head_grad + contract(grad_logits, normed_b, 0, 0), contract(grad_logits, emb_table, 1, 0)

            def grad_skip():
                return head_grad, jnp.zeros((seq_len, model_dim), jnp.float32)

            new_head, normed_part = lax.cond(is_last, grad_part, grad_skip)
            grad_normed = lax.psum(normed_part, 'tp')
            grad_top = (inv_rms * (grad_normed - normed * jnp.mean(normed * grad_normed, axis=-1, keepdims=True))).astype(jnp.bfloat16)
            return (loss_sum + jnp.sum(log_norm - target_logit), new_head), grad_top

        head_init = (jnp.zeros((), jnp.float32), jnp.zeros((vocab_rows, model_dim), jnp.float32))
        head_out, grad_tops = lax.scan(head_step, head_init, (y_top, lab_local))
        loss_sum, head_grad = head_out

        def bwd_tick(carry_in, tick_idx):
            g_recv, acc_one, acc_two, acc_table = carry_in
            micro_idx = tick_idx - (pp_size - 1 - stage_idx)
            is_valid = (micro_idx >= 0) & (micro_idx < num_micro)
            pick_idx = jnp.clip(micro_idx, 0, num_micro - 1)
            top_in = lax.dynamic_index_in_dim(grad_tops, pick_idx, 0, keepdims=False)
            grad_y = jnp.where(is_valid, jnp.where(is_last, top_in, g_recv), act_zero)
            x_act = lax.dynamic_index_in_dim(x_saved, pick_idx, 0, keepdims=False)
            hidden = lax.dynamic_index_in_dim(h_saved, pick_idx, 0, keepdims=False)
            gate_act, gelu_vjp = jax.vjp(jax.nn.gelu, hidden)
            grad_hidden = gelu_vjp(contract(grad_y, w_two, 1, 1))[0].astype(jnp.bfloat16)
            acc_two = acc_two + contract(gate_act.astype(jnp.bfloat16), grad_y, 0, 0)
            acc_one = acc_one + contract(x_act, grad_hidden, 0, 0)
            grad_x = (grad_y.astype(jnp.float32) + lax.psum(contract(grad_hidden, w_one, 1, 1), 'tp')).astype(jnp.bfloat16)
            tok_row = lax.dynamic_index_in_dim(tok_local, pick_idx, 0, keepdims=False)

            def add_rows():
                one_hot = (tok_row[:, None] == row_ids[None, :]).astype(jnp.bfloat16)
                return acc_table + contract(one_hot, grad_x, 0, 0)

            def keep_rows():
                return acc_table

            new_table = lax.cond(is_first, add_rows, keep_rows)
            return (lax.ppermute(grad_x, 'pp', bwd_perm), acc_one, acc_two, new_table), None

        bwd_init = (act_zero, jnp.zeros((model_dim, hidden_cols), jnp.float32), jnp.zeros((hidden_cols, model_dim), jnp.float32), jnp.zeros((vocab_rows, model_dim), jnp.float32))
        bwd_out = lax.scan(bwd_tick, bwd_init, jnp.arange(num_ticks))[0]
        grad_table = lax.psum(bwd_out[3] + head_grad, 'pp')
        mean_loss = lax.psum(jnp.where(is_last, loss_sum, 0.0), 'pp') / (num_micro * seq_len)
        return mean_loss.reshape(1), bwd_out[1][None], bwd_out[2][None], grad_table

    return jax.shard_map(device_fn, mesh=mesh, in_specs=(P('dp', None), P('dp', None), P('tp', None), P('pp', None, 'tp'), P('pp', 'tp', None)), out_specs=(P('dp'), P(('dp', 'pp'), None, 'tp'), P(('dp', 'pp'), 'tp', None), P(('dp', 'tp'), None)), check_vma=False)
```

profile of v0, /device:TPU:0, one launch (start us, length us, event | category | flops | bytes accessed | tf_op | source)
XLA Modules:
  0.0 6716.0 jit_solution(16882733202193195712)
XLA Ops:
  17.5 37.3 all-reduce.12.cloned.1.call-done
  54.9 342.1 %while.59 = (s32[]{:T(128)}, bf16[64,2048]{1,0:T(8,128)(2,1)S(1)}, bf16[7,64,2048]{2,1,0:T(8,128)(2,1)S(1)}, f32[7,64,4096]{2,1,0:T(8,128)}, bf16[7,64,2048]{2,1...) while((s32[]{:T(128)}, bf16[64,2048]{1,0:T(8,128)(2,1)S(1)}, ...), condition=%wide.region_3.4_spmd.clone, body=%wide.region_1.3_spmd.sunk.clone | while | flops 2150498304 | bytes 111150360 | solution.py:47
  116.6 28.0 all-reduce.16.cloned.1.call-done
  166.2 28.1 all-reduce.16.cloned.1.call-done
  215.8 28.1 all-reduce.16.cloned.1.call-done
  265.3 28.1 all-reduce.16.cloned.1.call-done
  314.9 28.1 all-reduce.16.cloned.1.call-done
  403.9 63.4 broadcast.111.clone
  467.3 1043.4 %while.60 = (s32[]{:T(128)}, f32[]{:T(128)}, f32[25136,2048]{1,0:T(8,128)}, bf16[4,64,2048]{2,1,0:T(8,128)(2,1)}, pred[]{:T(512)}, /*index=5*/bf16[4,64,2048]{2,...) while((s32[]{:T(128)}, f32[]{:T(128)}, ...), condition=%wide.region_19.20_spmd.clone.clone, body=%wide.region_4.19_spmd.clone.sunk.clone | while | flops 19843983360 | bytes 656755712 | solution.py:88
  483.9 241.9 %all-reduce.18.cloned.1.call-done = f32[64,2048]{1,0:T(8,128)} async-done(((f32[64,2048]{1,0:T(8,128)}), f32[64,2048]{1,0:T(8,128)}) %all-reduce.18.cloned.1.call-update) | async-done | bytes 524304 | tf_op jit(solution)/shard_map/while/body/eval_jaxpr/psum | solution.py:83
  745.6 240.7 %all-reduce.18.cloned.1.call-done = f32[64,2048]{1,0:T(8,128)} async-done(((f32[64,2048]{1,0:T(8,128)}), f32[64,2048]{1,0:T(8,128)}) %all-reduce.18.cloned.1.call-update) | async-done | bytes 524304 | tf_op jit(solution)/shard_map/while/body/eval_jaxpr/psum | solution.py:83
  1006.0 240.7 %all-reduce.18.cloned.1.call-done = f32[64,2048]{1,0:T(8,128)} async-done(((f32[64,2048]{1,0:T(8,128)}), f32[64,2048]{1,0:T(8,128)}) %all-reduce.18.cloned.1.call-update) | async-done | bytes 524304 | tf_op jit(solution)/shard_map/while/body/eval_jaxpr/psum | solution.py:83
  1266.5 240.7 %all-reduce.18.cloned.1.call-done = f32[64,2048]{1,0:T(8,128)} async-done(((f32[64,2048]{1,0:T(8,128)}), f32[64,2048]{1,0:T(8,128)}) %all-reduce.18.cloned.1.call-update) | async-done | bytes 524304 | tf_op jit(solution)/shard_map/while/body/eval_jaxpr/psum | solution.py:83
  1512.0 62.7 broadcast.111
  1574.7 1482.4 %while.61 = (s32[]{:T(128)}, bf16[64,2048]{1,0:T(8,128)(2,1)}, f32[2048,4096]{1,0:T(8,128)}, f32[4096,2048]{1,0:T(8,128)}, f32[25136,2048]{1,0:T(8,128)}, /*inde...) while((s32[]{:T(128)}, bf16[64,2048]{1,0:T(8,128)(2,1)}, ...), condition=%wide.region_25.26_spmd.clone.clone, body=%wide.region_21.25_spmd.clone.sunk.clone | while | flops 10979249152 | bytes 591075840 | solution.py:118
  1640.7 136.9 %conditional.14 = (f32[25136,2048]{1,0:T(8,128)}) conditional(s32[]{:T(128)} %convert_element_type.125, f32[25136,2048]{1,0:T(8,128)} %get-tuple-element.967, (s32[4,64]{1,0:T(4,128)}, s32[]{:T(128)}, s32[25136]{0:T(1024)S(1)}, bf16[64,2048]{1,0:T(8,128)(2,1)}, f32[25136,2048]{1,0:T(8,128)}) %tuple.132), branch_computations={%region_23.23_spmd, %region_24.24_spmd} | conditional | flops 6642338816 | bytes 412191680 | solution.py:114
  1641.4 136.2 %convolution_add_fusion.1 = f32[25136,2048]{1,0:T(8,128)} fusion(f32[25136,2048]{1,0:T(8,128)} %get-tuple-element.341, bf16[64,2048]{1,0:T(8,128)(2,1)} %get-tuple-element.345, s32[25136]{0:T(1024)S(1)} %get-tuple-element.344, s32[64]{0:T(128)S(1)} %dynamic-slice_bitcast_fusion), kind=kOutput, calls=%fused_computation.33 | convolution fusion | flops 6642338816 | bytes 412191168 | tf_op jit(solution)/shard_map/while/body/eval_jaxpr/cond/branch_1_fun/dot_general | solution.py:10
  1853.9 136.9 %conditional.14 = (f32[25136,2048]{1,0:T(8,128)}) conditional(s32[]{:T(128)} %convert_element_type.125, f32[25136,2048]{1,0:T(8,128)} %get-tuple-element.967, (s32[4,64]{1,0:T(4,128)}, s32[]{:T(128)}, s32[25136]{0:T(1024)S(1)}, bf16[64,2048]{1,0:T(8,128)(2,1)}, f32[25136,2048]{1,0:T(8,128)}) %tuple.132), branch_computations={%region_23.23_spmd, %region_24.24_spmd} | conditional | flops 6642338816 | bytes 412191680 | solution.py:114
  1854.6 136.2 %convolution_add_fusion.1 = f32[25136,2048]{1,0:T(8,128)} fusion(f32[25136,2048]{1,0:T(8,128)} %get-tuple-element.341, bf16[64,2048]{1,0:T(8,128)(2,1)} %get-tuple-element.345, s32[25136]{0:T(1024)S(1)} %get-tuple-element.344, s32[64]{0:T(128)S(1)} %dynamic-slice_bitcast_fusion), kind=kOutput, calls=%fused_computation.33 | convolution fusion | flops 6642338816 | bytes 412191168 | tf_op jit(solution)/shard_map/while/body/eval_jaxpr/cond/branch_1_fun/dot_general | solution.py:10
  2067.2 136.9 %conditional.14 = (f32[25136,2048]{1,0:T(8,128)}) conditional(s32[]{:T(128)} %convert_element_type.125, f32[25136,2048]{1,0:T(8,128)} %get-tuple-element.967, (s32[4,64]{1,0:T(4,128)}, s32[]{:T(128)}, s32[25136]{0:T(1024)S(1)}, bf16[64,2048]{1,0:T(8,128)(2,1)}, f32[25136,2048]{1,0:T(8,128)}) %tuple.132), branch_computations={%region_23.23_spmd, %region_24.24_spmd} | conditional | flops 6642338816 | bytes 412191680 | solution.py:114
  2067.9 136.2 %convolution_add_fusion.1 = f32[25136,2048]{1,0:T(8,128)} fusion(f32[25136,2048]{1,0:T(8,128)} %get-tuple-element.341, bf16[64,2048]{1,0:T(8,128)(2,1)} %get-tuple-element.345, s32[25136]{0:T(1024)S(1)} %get-tuple-element.344, s32[64]{0:T(128)S(1)} %dynamic-slice_bitcast_fusion), kind=kOutput, calls=%fused_computation.33 | convolution fusion | flops 6642338816 | bytes 412191168 | tf_op jit(solution)/shard_map/while/body/eval_jaxpr/cond/branch_1_fun/dot_general | solution.py:10
  2280.4 136.9 %conditional.14 = (f32[25136,2048]{1,0:T(8,128)}) conditional(s32[]{:T(128)} %convert_element_type.125, f32[25136,2048]{1,0:T(8,128)} %get-tuple-element.967, (s32[4,64]{1,0:T(4,128)}, s32[]{:T(128)}, s32[25136]{0:T(1024)S(1)}, bf16[64,2048]{1,0:T(8,128)(2,1)}, f32[25136,2048]{1,0:T(8,128)}) %tuple.132), branch_computations={%region_23.23_spmd, %region_24.24_spmd} | conditional | flops 6642338816 | bytes 412191680 | solution.py:114
  2281.1 136.2 %convolution_add_fusion.1 = f32[25136,2048]{1,0:T(8,128)} fusion(f32[25136,2048]{1,0:T(8,128)} %get-tuple-element.341, bf16[64,2048]{1,0:T(8,128)(2,1)} %get-tuple-element.345, s32[25136]{0:T(1024)S(1)} %get-tuple-element.344, s32[64]{0:T(128)S(1)} %dynamic-slice_bitcast_fusion), kind=kOutput, calls=%fused_computation.33 | convolution fusion | flops 6642338816 | bytes 412191168 | tf_op jit(solution)/shard_map/while/body/eval_jaxpr/cond/branch_1_fun/dot_general | solution.py:10
  2493.7 136.9 %conditional.14 = (f32[25136,2048]{1,0:T(8,128)}) conditional(s32[]{:T(128)} %convert_element_type.125, f32[25136,2048]{1,0:T(8,128)} %get-tuple-element.967, (s32[4,64]{1,0:T(4,128)}, s32[]{:T(128)}, s32[25136]{0:T(1024)S(1)}, bf16[64,2048]{1,0:T(8,128)(2,1)}, f32[25136,2048]{1,0:T(8,128)}) %tuple.132), branch_computations={%region_23.23_spmd, %region_24.24_spmd} | conditional | flops 6642338816 | bytes 412191680 | solution.py:114
  2494.4 136.2 %convolution_add_fusion.1 = f32[25136,2048]{1,0:T(8,128)} fusion(f32[25136,2048]{1,0:T(8,128)} %get-tuple-element.341, bf16[64,2048]{1,0:T(8,128)(2,1)} %get-tuple-element.345, s32[25136]{0:T(1024)S(1)} %get-tuple-element.344, s32[64]{0:T(128)S(1)} %dynamic-slice_bitcast_fusion), kind=kOutput, calls=%fused_computation.33 | convolution fusion | flops 6642338816 | bytes 412191168 | tf_op jit(solution)/shard_map/while/body/eval_jaxpr/cond/branch_1_fun/dot_general | solution.py:10
  2706.9 136.9 %conditional.14 = (f32[25136,2048]{1,0:T(8,128)}) conditional(s32[]{:T(128)} %convert_element_type.125, f32[25136,2048]{1,0:T(8,128)} %get-tuple-element.967, (s32[4,64]{1,0:T(4,128)}, s32[]{:T(128)}, s32[25136]{0:T(1024)S(1)}, bf16[64,2048]{1,0:T(8,128)(2,1)}, f32[25136,2048]{1,0:T(8,128)}) %tuple.132), branch_computations={%region_23.23_spmd, %region_24.24_spmd} | conditional | flops 6642338816 | bytes 412191680 | solution.py:114
  2707.6 136.2 %convolution_add_fusion.1 = f32[25136,2048]{1,0:T(8,128)} fusion(f32[25136,2048]{1,0:T(8,128)} %get-tuple-element.341, bf16[64,2048]{1,0:T(8,128)(2,1)} %get-tuple-element.345, s32[25136]{0:T(1024)S(1)} %get-tuple-element.344, s32[64]{0:T(128)S(1)} %dynamic-slice_bitcast_fusion), kind=kOutput, calls=%fused_computation.33 | convolution fusion | flops 6642338816 | bytes 412191168 | tf_op jit(solution)/shard_map/while/body/eval_jaxpr/cond/branch_1_fun/dot_general | solution.py:10
  2920.2 136.9 %conditional.14 = (f32[25136,2048]{1,0:T(8,128)}) conditional(s32[]{:T(128)} %convert_element_type.125, f32[25136,2048]{1,0:T(8,128)} %get-tuple-element.967, (s32[4,64]{1,0:T(4,128)}, s32[]{:T(128)}, s32[25136]{0:T(1024)S(1)}, bf16[64,2048]{1,0:T(8,128)(2,1)}, f32[25136,2048]{1,0:T(8,128)}) %tuple.132), branch_computations={%region_23.23_spmd, %region_24.24_spmd} | conditional | flops 6642338816 | bytes 412191680 | solution.py:114
  2920.9 136.2 %convolution_add_fusion.1 = f32[25136,2048]{1,0:T(8,128)} fusion(f32[25136,2048]{1,0:T(8,128)} %get-tuple-element.341, bf16[64,2048]{1,0:T(8,128)(2,1)} %get-tuple-element.345, s32[25136]{0:T(1024)S(1)} %get-tuple-element.344, s32[64]{0:T(128)S(1)} %dynamic-slice_bitcast_fusion), kind=kOutput, calls=%fused_computation.33 | convolution fusion | flops 6642338816 | bytes 412191168 | tf_op jit(solution)/shard_map/while/body/eval_jaxpr/cond/branch_1_fun/dot_general | solution.py:10
  3057.1 192.6 %add.115 = f32[25136,2048]{1,0:T(8,128)} add(f32[25136,2048]{1,0:T(8,128)} %get-tuple-element.383, f32[25136,2048]{1,0:T(8,128)} %get-tuple-element.384) | non-fusion elementwise | flops 51478528 | bytes 617742336 | tf_op jit(solution)/shard_map/add | solution.py:119
  3257.1 3316.1 %all-reduce.14.cloned.1.call-done = f32[25136,2048]{1,0:T(8,128)} async-done(((f32[25136,2048]{1,0:T(8,128)}), f32[25136,2048]{1,0:T(8,128)}) %all-reduce.14.cloned.1.call-update) | async-done | bytes 205914128 | tf_op jit(solution)/shard_map/psum | solution.py:119
  6573.3 134.4 %copy.78 = f32[25136,2048]{1,0:T(8,128)} copy(f32[25136,2048]{1,0:T(8,128)} %all-reduce.14.cloned.1.call-done) | data formatting | bytes 411828224
  (341 shorter events, 835.1 us)
Async XLA Ops:
  7.2 47.7 all-reduce.12.cloned.1.call-start
  54.9 40.1 all-reduce.16.cloned.1.call-start
  96.9 2.6 collective-permute-start
  99.5 45.1 all-reduce.16.cloned.1.call-start
  146.5 2.6 collective-permute-start
  149.1 45.1 all-reduce.16.cloned.1.call-start
  196.0 2.6 collective-permute-start
  198.7 45.1 all-reduce.16.cloned.1.call-start
  245.6 2.6 collective-permute-start
  248.3 45.1 all-reduce.16.cloned.1.call-start
  297.9 45.1 all-reduce.16.cloned.1.call-start
  347.5 45.1 all-reduce.16.cloned.1.call-start
  394.4 2.6 collective-permute-start
  467.5 258.4 %all-reduce.18.cloned.1.call-start = ((), (), s32[]{:S(2)}) async-start(), calls=%async_computation.3 | async-start | bytes 1048576 | tf_op jit(solution)/shard_map/while/body/eval_jaxpr/psum | solution.py:83
  729.2 257.1 %all-reduce.18.cloned.1.call-start = ((), (), s32[]{:S(2)}) async-start(), calls=%async_computation.3 | async-start | bytes 1048576 | tf_op jit(solution)/shard_map/while/body/eval_jaxpr/psum | solution.py:83
  989.6 257.1 %all-reduce.18.cloned.1.call-start = ((), (), s32[]{:S(2)}) async-start(), calls=%async_computation.3 | async-start | bytes 1048576 | tf_op jit(solution)/shard_map/while/body/eval_jaxpr/psum | solution.py:83
  1250.1 257.1 %all-reduce.18.cloned.1.call-start = ((), (), s32[]{:S(2)}) async-start(), calls=%async_computation.3 | async-start | bytes 1048576 | tf_op jit(solution)/shard_map/while/body/eval_jaxpr/psum | solution.py:83
  1574.7 49.2 all-reduce.20.cloned.1.call-start
  1625.6 151.9 %collective-permute-start.1 = (bf16[64,2048]{1,0:T(8,128)(2,1)}, bf16[64,2048]{1,0:T(8,128)(2,1)}, u32[]{:S(2)}, u32[]{:S(2)}) collective-permute-start(bf16[64,2048]{1,0:T(8,128)(2,1)} %add_convert_fusion.5), channel_id=1, source_target_pairs={{1,0},{2,1},{3,2},{5,4},{6,5},{7,6}} | collective-permute-start | bytes 786440 | tf_op jit(solution)/shard_map/while/body/eval_jaxpr/ppermute | solution.py:115
  1777.6 51.2 all-reduce.20.cloned.1.call-start
  1830.6 160.2 %collective-permute-start.1 = (bf16[64,2048]{1,0:T(8,128)(2,1)}, bf16[64,2048]{1,0:T(8,128)(2,1)}, u32[]{:S(2)}, u32[]{:S(2)}) collective-permute-start(bf16[64,2048]{1,0:T(8,128)(2,1)} %add_convert_fusion.5), channel_id=1, source_target_pairs={{1,0},{2,1},{3,2},{5,4},{6,5},{7,6}} | collective-permute-start | bytes 786440 | tf_op jit(solution)/shard_map/while/body/eval_jaxpr/ppermute | solution.py:115
  1990.8 51.3 all-reduce.20.cloned.1.call-start
  2043.9 160.2 %collective-permute-start.1 = (bf16[64,2048]{1,0:T(8,128)(2,1)}, bf16[64,2048]{1,0:T(8,128)(2,1)}, u32[]{:S(2)}, u32[]{:S(2)}) collective-permute-start(bf16[64,2048]{1,0:T(8,128)(2,1)} %add_convert_fusion.5), channel_id=1, source_target_pairs={{1,0},{2,1},{3,2},{5,4},{6,5},{7,6}} | collective-permute-start | bytes 786440 | tf_op jit(solution)/shard_map/while/body/eval_jaxpr/ppermute | solution.py:115
  2204.1 51.2 all-reduce.20.cloned.1.call-start
  2257.1 160.2 %collective-permute-start.1 = (bf16[64,2048]{1,0:T(8,128)(2,1)}, bf16[64,2048]{1,0:T(8,128)(2,1)}, u32[]{:S(2)}, u32[]{:S(2)}) collective-permute-start(bf16[64,2048]{1,0:T(8,128)(2,1)} %add_convert_fusion.5), channel_id=1, source_target_pairs={{1,0},{2,1},{3,2},{5,4},{6,5},{7,6}} | collective-permute-start | bytes 786440 | tf_op jit(solution)/shard_map/while/body/eval_jaxpr/ppermute | solution.py:115
  2417.3 51.3 all-reduce.20.cloned.1.call-start
  2470.4 160.2 %collective-permute-start.1 = (bf16[64,2048]{1,0:T(8,128)(2,1)}, bf16[64,2048]{1,0:T(8,128)(2,1)}, u32[]{:S(2)}, u32[]{:S(2)}) collective-permute-start(bf16[64,2048]{1,0:T(8,128)(2,1)} %add_convert_fusion.5), channel_id=1, source_target_pairs={{1,0},{2,1},{3,2},{5,4},{6,5},{7,6}} | collective-permute-start | bytes 786440 | tf_op jit(solution)/shard_map/while/body/eval_jaxpr/ppermute | solution.py:115
  2630.5 51.2 all-reduce.20.cloned.1.call-start
  2683.6 160.2 %collective-permute-start.1 = (bf16[64,2048]{1,0:T(8,128)(2,1)}, bf16[64,2048]{1,0:T(8,128)(2,1)}, u32[]{:S(2)}, u32[]{:S(2)}) collective-permute-start(bf16[64,2048]{1,0:T(8,128)(2,1)} %add_convert_fusion.5), channel_id=1, source_target_pairs={{1,0},{2,1},{3,2},{5,4},{6,5},{7,6}} | collective-permute-start | bytes 786440 | tf_op jit(solution)/shard_map/while/body/eval_jaxpr/ppermute | solution.py:115
  2843.8 51.3 all-reduce.20.cloned.1.call-start
  2896.8 160.2 %collective-permute-start.1 = (bf16[64,2048]{1,0:T(8,128)(2,1)}, bf16[64,2048]{1,0:T(8,128)(2,1)}, u32[]{:S(2)}, u32[]{:S(2)}) collective-permute-start(bf16[64,2048]{1,0:T(8,128)(2,1)} %add_convert_fusion.5), channel_id=1, source_target_pairs={{1,0},{2,1},{3,2},{5,4},{6,5},{7,6}} | collective-permute-start | bytes 786440 | tf_op jit(solution)/shard_map/while/body/eval_jaxpr/ppermute | solution.py:115
  3057.0 3516.2 %all-reduce.14.cloned.1.call-start = ((), (), s32[]{:S(2)}) async-start(), calls=%async_computation.1 | async-start | bytes 411828224 | tf_op jit(solution)/shard_map/psum | solution.py:119
  (28 other events, 2077.5 us)
Sparse Core Ops, SparseCore 0:
  17.6 37.2 all-reduce.11
  72.2 22.8 all-reduce.15
  116.7 27.8 all-reduce.15
  166.3 27.8 all-reduce.15
  215.9 27.8 all-reduce.15
  265.5 27.8 all-reduce.15
  315.1 27.8 all-reduce.15
  364.7 27.8 all-reduce.15
  483.4 242.4 all-reduce.17
  745.0 241.2 all-reduce.17
  1005.5 241.2 all-reduce.17
  1265.9 241.2 all-reduce.17
  1601.0 22.8 all-reduce.19
  1803.9 21.7 all-reduce.19
  2017.2 21.7 all-reduce.19
  2230.4 21.6 all-reduce.19
  2443.6 21.7 all-reduce.19
  2656.9 21.7 all-reduce.19
  2870.1 21.7 all-reduce.19
  3249.9 3323.3 all-reduce.13
where the time goes:
time: 6730 us; the launch traced here: 6720 us
  waiting for transfers between devices  4530 us (67%)
  matrix products  1520 us (23%)
  local copies, waits for them, and re-layouts  326 us (5%)
  other arithmetic  263 us (4%)
    psum x1, waiting for transfers between devices, device_fn(): grad_table = lax.psum(bwd_out[3] + head_grad, 'pp')  3320 us
    dot_general x35, matrix products, contract(): lax.dot_general(lhs, rhs, (((lhs_dim,), (rhs_dim,)), ((), ())), preferred...  1430 us
    psum x4, waiting for transfers between devices, head_step(): grad_normed = lax.psum(normed_part, 'tp')  964 us
    add x1, other arithmetic, device_fn(): grad_table = lax.psum(bwd_out[3] + head_grad, 'pp')  193 us
    psum x7, waiting for transfers between devices, fwd_tick(): lax.psum(jnp.dot(gate_act, w_two, preferred_element_type=jnp.float32), 'tp')  191 us
    another operation x18, local copies, waits for them, and re-layouts  142 us
    unnamed x7, local copies, waits for them, and re-layouts  135 us
  transfers between devices with their start and end apart: 34, of which 21 were waited for; matrix products, arithmetic and copies ran while one was open for 19% of the time, Pallas kernels for 0%

commit v1 on v0

v1 whole, which is shorter than its diff:
```python
import jax
import jax.numpy as jnp
from jax import lax
from jax.sharding import PartitionSpec as P

NORM_EPS = 1e-6
AXES = ('tp', 'pp')


def contract(lhs, rhs, lhs_dim, rhs_dim):
    return lax.dot_general(lhs, rhs, (((lhs_dim,), (rhs_dim,)), ((), ())), preferred_element_type=jnp.float32)


def solution(mesh):
    pp_size = mesh.shape['pp']
    last = pp_size - 1

    def link(src_stage, dst_stage, cross):
        return [(t * pp_size + src_stage, (1 - t if cross else t) * pp_size + dst_stage) for t in range(2)]

    def send(value, src_stage, dst_stage, cross):
        return lax.ppermute(value, AXES, link(src_stage, dst_stage, cross))

    def device_fn(tokens, labels, emb_table, w_in, w_out):
        num_micro, seq_len = tokens.shape
        num_tok = num_micro * seq_len
        half = num_tok // 2
        vocab_rows, model_dim = emb_table.shape
        w_one = w_in[0]
        w_two = w_out[0]
        stage_idx = lax.axis_index('pp')
        tp_idx = lax.axis_index('tp')
        is_low = tp_idx == 0
        vocab_base = tp_idx * vocab_rows
        tok_local = tokens.reshape(num_tok) - vocab_base
        lab_local = labels.reshape(num_tok) - vocab_base
        row_ids = jnp.arange(vocab_rows, dtype=jnp.int32)

        def mine(value):
            return lax.dynamic_slice_in_dim(value, tp_idx * half, half, 0)

        def theirs(value):
            return lax.dynamic_slice_in_dim(value, (1 - tp_idx) * half, half, 0)

        def join(own, other):
            return jnp.concatenate([jnp.where(is_low, own, other), jnp.where(is_low, other, own)], axis=0)

        def reduce_half(partial, stage):
            return mine(partial) + send(theirs(partial), stage, stage, True)

        owned = (tok_local >= 0) & (tok_local < vocab_rows)
        looked_up = jnp.take(emb_table, jnp.clip(tok_local, 0, vocab_rows - 1), axis=0)
        looked_up = jnp.where(owned[:, None], looked_up, jnp.zeros_like(looked_up))
        x_act = looked_up + send(looked_up, 0, 0, True)

        for stage in range(pp_size):
            hidden = jnp.dot(x_act, w_one, preferred_element_type=jnp.float32)
            gate_act = jax.nn.gelu(hidden).astype(jnp.bfloat16)
            branch = reduce_half(jnp.dot(gate_act, w_two, preferred_element_type=jnp.float32), stage)
            y_half = (mine(x_act).astype(jnp.float32) + branch).astype(jnp.bfloat16)
            if stage < last:
                arrived = join(send(y_half, stage, stage + 1, False), send(y_half, stage, stage + 1, True))
                x_act = jnp.where(stage_idx == stage + 1, arrived, x_act)

        y_pair = join(y_half, send(y_half, last, last, True))
        y_mid = send(y_pair, last, 1, False)
        y_rest = send(y_pair, last, 2, False) + y_mid + send(y_mid, 1, 0, False)
        y_top = jnp.where(stage_idx == last, y_pair, y_rest)

        x_wide = y_top.astype(jnp.float32)
        inv_rms = lax.rsqrt(jnp.mean(x_wide * x_wide, axis=-1, keepdims=True) + NORM_EPS)
        normed = x_wide * inv_rms
        normed_b = normed.astype(jnp.bfloat16)
        logits = contract(emb_table, normed_b, 1, 1)
        target_hit = row_ids[:, None] == lab_local[None, :]
        local_max = jnp.max(logits, axis=0)
        local_sum = jnp.sum(jnp.exp(logits - local_max[None, :]), axis=0)
        local_target = jnp.sum(jnp.where(target_hit, logits, 0.0), axis=0)
        stats = jnp.stack([jnp.log(local_sum) + local_max, local_target])
        other = lax.ppermute(stats, 'tp', [(0, 1), (1, 0)])
        log_norm = jnp.logaddexp(stats[0], other[0])
        mean_loss = jnp.sum(log_norm - (stats[1] + other[1])) / num_tok
        grad_logits = (jnp.exp(logits - log_norm[None, :]) - target_hit.astype(jnp.float32)).astype(jnp.bfloat16)
        grad_normed = reduce_half(contract(grad_logits, emb_table, 0, 0), last)
        normed_h = mine(normed)
        grad_half = (mine(inv_rms) * (grad_normed - normed_h * jnp.mean(normed_h * grad_normed, axis=-1, keepdims=True))).astype(jnp.bfloat16)
        grad_y = join(grad_half, send(grad_half, last, last, True))

        gelu_vjp = jax.vjp(jax.nn.gelu, hidden)[1]
        for stage in range(last, -1, -1):
            grad_hidden = gelu_vjp(contract(grad_y, w_two, 1, 1))[0].astype(jnp.bfloat16)
            branch = reduce_half(contract(grad_hidden, w_one, 1, 1), stage)
            dx_half = (mine(grad_y).astype(jnp.float32) + branch).astype(jnp.bfloat16)
            if stage > 0:
                arrived = join(send(dx_half, stage, stage - 1, False), send(dx_half, stage, stage - 1, True))
                grad_y = jnp.where(stage_idx == stage - 1, arrived, grad_y)

        dx_pair = join(dx_half, send(dx_half, 0, 0, True))
        dx_mid = send(dx_pair, 0, 2, False)
        dx_rest = send(dx_pair, 0, 1, False) + dx_mid + send(dx_mid, 2, 3, False)
        dx_rows = jnp.where(stage_idx == 0, dx_pair, dx_rest)

        grad_two = contract(gate_act, grad_y, 0, 0)
        grad_one = contract(x_act, grad_hidden, 0, 0)
        token_hit = (row_ids[:, None] == tok_local[None, :]).astype(jnp.bfloat16)
        table_lhs = jnp.concatenate([grad_logits, token_hit], axis=1)
        grad_table = contract(table_lhs, jnp.concatenate([normed_b, dx_rows], axis=0), 1, 0)
        return mean_loss.reshape(1), grad_one[None], grad_two[None], grad_table

    return jax.shard_map(device_fn, mesh=mesh, in_specs=(P('dp', None), P('dp', None), P('tp', None), P('pp', None, 'tp'), P('pp', 'tp', None)), out_specs=(P('dp'), P(('dp', 'pp'), None, 'tp'), P(('dp', 'pp'), 'tp', None), P(('dp', 'tp'), None)), check_vma=False)
```

time: 6730 us -> 716 us (0.11)
  waiting for transfers between devices: 4530 us -> 243 us
  matrix products: 1520 us -> 348 us
  local copies, waits for them, and re-layouts: 326 us -> 16.2 us
  other arithmetic: 263 us -> 54 us
    psum x20 -> x0, waiting for transfers between devices: 4520 us -> none  [the longest x1 3320 us: device_fn(): grad_table = lax.psum(bwd_out[3] + head_grad, 'pp')]
    dot_general x35 -> x13, matrix products: 1430 us -> 286 us  [contract(): lax.dot_general(lhs, rhs, (((lhs_dim,), (rhs_dim,)), ((), ())), preferred...]
    ppermute x14 -> x32, waiting for transfers between devices: 7.89 us -> 243 us  [the longest x31 239 us: send(): return lax.ppermute(value, AXES, link(src_stage, dst_stage, cross))]
    add x1 -> x2, other arithmetic: 193 us -> 0.25 us  [the longest x1 0.25 us: device_fn(): x_act = looked_up + send(looked_up, 0, 0, True)]
    another operation x18 -> x1, local copies, waits for them, and re-layouts: 142 us -> 0.08 us
    unnamed x7 -> x50, local copies, waits for them, and re-layouts: 135 us -> 2.43 us
  transfers between devices with their start and end apart: 34 -> 32, of which waited for: 21 -> 9; matrix products, arithmetic and copies ran while one was open for 19% -> 6% of each run, Pallas kernels for 0% -> 0%
where the time goes in v1:
time: 716 us; the launch traced here: 709 us
  matrix products  348 us (49%)
  waiting for transfers between devices  243 us (34%)
  other arithmetic  54 us (8%)
  starting transfers between devices  44.8 us (6%)
  local copies, waits for them, and re-layouts  16.2 us (2%)
    dot_general x13, matrix products, contract(): lax.dot_general(lhs, rhs, (((lhs_dim,), (rhs_dim,)), ((), ())), preferred...  286 us
    ppermute x31, waiting for transfers between devices, send(): return lax.ppermute(value, AXES, link(src_stage, dst_stage, cross))  239 us
    dot_general x4, matrix products, device_fn(): jnp.dot(gate_act, w_two, preferred_element_type=jnp.float32)  53.1 us
    ppermute x31, starting transfers between devices, send(): return lax.ppermute(value, AXES, link(src_stage, dst_stage, cross))  44.5 us
  transfers between devices with their start and end apart: 32, of which 9 were waited for; matrix products, arithmetic and copies ran while one was open for 6% of the time, Pallas kernels for 0%

profile of v1, /device:TPU:0, one launch (start us, length us, event | category | flops | bytes accessed | tf_op | source)
XLA Modules:
  0.0 709.4 jit_solution(86721297968782535)
XLA Ops:
  2.0 7.8 %gather_fusion = bf16[256,2048]{1,0:T(8,128)(2,1)S(1)} fusion(bf16[25136,2048]{1,0:T(8,128)(2,1)} %param.7, s32[1024]{0:T(1024)S(1)} %pad_clamp_fusion), kind=kCustom, calls=%fused_computation | custom fusion | bytes 2098176 | tf_op jit(solution)/shard_map/jit(_take)/gather | solution.py:52
  10.0 5.2 collective-permute-start
  15.3 12.8 %collective-permute-done = bf16[256,2048]{1,0:T(8,128)(2,1)S(1)} collective-permute-done((bf16[256,2048]{1,0:T(8,128)(2,1)S(1)}, bf16[256,2048]{1,0:T(8,128)(2,1)S(1)}, u32[]{:S(2)}, u32[]{:S(2)}) %collective-permute-start) | collective-permute-done | bytes 1048608 | tf_op jit(solution)/shard_map/ppermute | solution.py:22
  28.3 16.5 %fusion.25 = f32[256,2048]{1,0:T(8,128)} fusion(bf16[1,4096,2048]{2,1,0:T(8,128)(2,1)} %param.9, bf16[256,2048]{1,0:T(8,128)(2,1)S(1)} %fusion.148, bf16[1,2048,4096]{2,1,0:T(8,128)(2,1)} %param.8), kind=kOutput, calls=%fused_computation.33 | convolution fusion | flops 8599371776 | bytes 36700160 | tf_op jit(solution)/shard_map/dot_general | solution.py:59
  46.1 3.9 collective-permute-start.1
  50.1 12.8 %collective-permute-done.1 = f32[128,2048]{1,0:T(8,128)S(1)} collective-permute-done((f32[128,2048]{1,0:T(8,128)S(1)}, f32[128,2048]{1,0:T(8,128)S(1)}, u32[]{:S(2)}, u32[]{:S(2)}) %collective-permute-start.1) | collective-permute-done | bytes 1048608 | tf_op jit(solution)/shard_map/ppermute | solution.py:22
  67.8 6.4 collective-permute-done.3
  74.7 15.2 %fusion.23 = f32[256,2048]{1,0:T(8,128)S(1)} fusion(bf16[1,4096,2048]{2,1,0:T(8,128)(2,1)} %param.9, bf16[256,2048]{1,0:T(8,128)(2,1)S(1)} %maximum_select_fusion, bf16[1,2048,4096]{2,1,0:T(8,128)(2,1)} %param.8), kind=kOutput, calls=%fused_computation.31 | convolution fusion | flops 8599371776 | bytes 36700160 | tf_op jit(solution)/shard_map/dot_general | solution.py:59
  93.7 16.5 %fusion.21 = f32[256,2048]{1,0:T(8,128)} fusion(bf16[1,4096,2048]{2,1,0:T(8,128)(2,1)} %param.9, bf16[256,2048]{1,0:T(8,128)(2,1)S(1)} %maximum_select_fusion.1, bf16[1,2048,4096]{2,1,0:T(8,128)(2,1)} %param.8), kind=kOutput, calls=%fused_computation.29 | convolution fusion | flops 8599371776 | bytes 36700160 | tf_op jit(solution)/shard_map/dot_general | solution.py:59
  115.9 8.7 %fusion.35 = f32[256,4096]{1,0:T(8,128)S(1)} fusion(bf16[256,2048]{1,0:T(8,128)(2,1)S(1)} %maximum_select_fusion.2, bf16[1,2048,4096]{2,1,0:T(8,128)(2,1)} %param.8), kind=kOutput, calls=%fused_computation.43 | convolution fusion | flops 4294967296 | bytes 22020096 | tf_op jit(solution)/shard_map/dot_general | solution.py:57
  126.5 4.9 fusion.19
  137.4 92.9 %collective-permute-done.14 = bf16[256,2048]{1,0:T(8,128)(2,1)} collective-permute-done((bf16[256,2048]{1,0:T(8,128)(2,1)S(1)}, bf16[256,2048]{1,0:T(8,128)(2,1)}, u32[]{:S(2)}, u32[]{:S(2)}) %collective-permute-start.14) | collective-permute-done | bytes 1048608 | tf_op jit(solution)/shard_map/ppermute | solution.py:22
  234.2 50.0 %fusion.128 = (f32[256]{0:T(256)S(1)}, f32[256,25136]{0,1:T(8,128)}) fusion(bf16[256,2048]{1,0:T(8,128)(2,1)S(1)} %get-tuple-element.11, bf16[25136,2048]{1,0:T(8,128)(2,1)} %param.7), kind=kOutput, calls=%fused_computation.190 | convolution fusion | flops 26363441152 | bytes 129745920 | tf_op jit(solution)/shard_map/dot_general | solution.py:11
  284.2 13.2 %fusion.5 = (f32[256]{0:T(256)S(1)}, f32[256]{0:T(256)S(1)}) fusion(f32[256,25136]{0,1:T(8,128)} %get-tuple-element.36, f32[256]{0:T(256)S(1)} %get-tuple-element.35, s32[256]{0:T(256)S(1)} %sub.91), kind=kLoop, calls=%fused_computation.9 | loop fusion | flops 32173568 | bytes 25743360 | tf_op jit(solution)/shard_map/reduce_sum | solution.py:77
  301.7 8.4 %fusion.9 = bf16[25136,256]{1,0:T(8,128)(2,1)} fusion(f32[256,25136]{0,1:T(8,128)S(1)} %copy-done, f32[256]{0:T(256)S(1)} %bitcast.108, s32[256]{0:T(256)S(1)} %sub.91), kind=kLoop, calls=%fused_computation.13 | loop fusion | flops 32174080 | bytes 38610944 | tf_op jit(solution)/shard_map/convert_element_type | solution.py:83
  310.1 40.9 %fusion.129 = f32[256,2048]{1,0:T(8,128)S(1)} fusion(bf16[25136,256]{1,0:T(8,128)(2,1)} %fusion.9, bf16[25136,2048]{1,0:T(8,128)(2,1)} %param.7), kind=kOutput, calls=%fused_computation.191 | convolution fusion | flops 26357006336 | bytes 117923840 | tf_op jit(solution)/shard_map/dot_general | solution.py:11
  355.2 11.3 %add_convert_fusion.3 = bf16[256,4096]{1,0:T(8,128)(2,1)} fusion(f32[256,4096]{1,0:T(8,128)S(1)} %copy-done.3, bf16[1,4096,2048]{2,1,0:T(8,128)(2,1)} %param.9, bf16[128,2048]{1,0:T(8,128)(2,1)S(1)} %get-tuple-element.21, bf16[128,2048]{1,0:T(8,128)(2,1)S(1)} %get-tuple-element.20), kind=kOutput, calls=%fused_computation.87 | convolution fusion | flops 4318035968 | bytes 24117248 | tf_op jit(solution)/shard_map/dot_general | solution.py:11
  366.5 8.7 %fusion.33 = f32[256,2048]{1,0:T(8,128)S(1)} fusion(bf16[256,4096]{1,0:T(8,128)(2,1)} %add_convert_fusion.3, bf16[1,2048,4096]{2,1,0:T(8,128)(2,1)} %param.8), kind=kOutput, calls=%fused_computation.41 | convolution fusion | flops 4294967296 | bytes 20971520 | tf_op jit(solution)/shard_map/dot_general | solution.py:11
  378.7 11.2 %add_convert_fusion.2 = bf16[256,4096]{1,0:T(8,128)(2,1)} fusion(f32[256,4096]{1,0:T(8,128)S(1)} %copy-done.4, bf16[256,2048]{1,0:T(8,128)(2,1)S(1)} %maximum_select_fusion.3, bf16[1,4096,2048]{2,1,0:T(8,128)(2,1)} %param.9), kind=kOutput, calls=%fused_computation.86 | convolution fusion | flops 4315938816 | bytes 24117248 | tf_op jit(solution)/shard_map/dot_general | solution.py:11
  389.9 12.2 %fusion.31 = f32[256,2048]{1,0:T(8,128)} fusion(bf16[256,4096]{1,0:T(8,128)(2,1)} %add_convert_fusion.2, bf16[1,2048,4096]{2,1,0:T(8,128)(2,1)} %param.8), kind=kOutput, calls=%fused_computation.39 | convolution fusion | flops 4294967296 | bytes 20971520 | tf_op jit(solution)/shard_map/dot_general | solution.py:11
  408.2 11.2 %add_convert_fusion.1 = bf16[256,4096]{1,0:T(8,128)(2,1)} fusion(f32[256,4096]{1,0:T(8,128)S(1)} %copy-done.5, bf16[256,2048]{1,0:T(8,128)(2,1)S(1)} %maximum_select_fusion.4, bf16[1,4096,2048]{2,1,0:T(8,128)(2,1)} %param.9), kind=kOutput, calls=%fused_computation.85 | convolution fusion | flops 4315938816 | bytes 24117248 | tf_op jit(solution)/shard_map/dot_general | solution.py:11
  419.4 8.7 %fusion.29 = f32[256,2048]{1,0:T(8,128)S(1)} fusion(bf16[256,4096]{1,0:T(8,128)(2,1)} %add_convert_fusion.1, bf16[1,2048,4096]{2,1,0:T(8,128)(2,1)} %param.8), kind=kOutput, calls=%fused_computation.37 | convolution fusion | flops 4294967296 | bytes 20971520 | tf_op jit(solution)/shard_map/dot_general | solution.py:11
  432.9 87.2 %collective-permute-done.25 = bf16[128,2048]{1,0:T(8,128)(2,1)S(1)} collective-permute-done((bf16[128,2048]{1,0:T(8,128)(2,1)}, bf16[128,2048]{1,0:T(8,128)(2,1)S(1)}, u32[]{:S(2)}, u32[]{:S(2)}) %collective-permute-start.25) | collective-permute-done | bytes 524320 | tf_op jit(solution)/shard_map/ppermute | solution.py:22
  520.0 6.7 collective-permute-done.26
  527.2 11.2 %add_convert_fusion = bf16[256,4096]{1,0:T(8,128)(2,1)} fusion(f32[256,4096]{1,0:T(8,128)S(1)} %copy-done.6, bf16[256,2048]{1,0:T(8,128)(2,1)S(1)} %maximum_select_fusion.5, bf16[1,4096,2048]{2,1,0:T(8,128)(2,1)} %param.9), kind=kOutput, calls=%fused_computation.84 | convolution fusion | flops 4315938816 | bytes 24117248 | tf_op jit(solution)/shard_map/dot_general | solution.py:11
  538.4 12.2 %fusion.27 = f32[256,2048]{1,0:T(8,128)} fusion(bf16[256,4096]{1,0:T(8,128)(2,1)} %add_convert_fusion, bf16[1,2048,4096]{2,1,0:T(8,128)(2,1)} %param.8), kind=kOutput, calls=%fused_computation.35 | convolution fusion | flops 4294967296 | bytes 20971520 | tf_op jit(solution)/shard_map/dot_general | solution.py:11
  555.6 13.1 %collective-permute-done.27 = f32[128,2048]{1,0:T(8,128)S(1)} collective-permute-done((f32[128,2048]{1,0:T(8,128)S(1)}, f32[128,2048]{1,0:T(8,128)S(1)}, u32[]{:S(2)}, u32[]{:S(2)}) %collective-permute-start.27) | collective-permute-done | bytes 1048608 | tf_op jit(solution)/shard_map/ppermute | solution.py:22
  573.7 7.4 %collective-permute-done.28 = bf16[128,2048]{1,0:T(8,128)(2,1)S(1)} collective-permute-done((bf16[128,2048]{1,0:T(8,128)(2,1)S(1)}, bf16[128,2048]{1,0:T(8,128)(2,1)S(1)}, u32[]{:S(2)}, u32[]{:S(2)}) %collective-permute-start.28) | collective-permute-done | bytes 524320 | tf_op jit(solution)/shard_map/ppermute | solution.py:22
  584.8 8.5 %fusion.10 = bf16[25136,256]{1,0:T(8,128)(2,1)} fusion(s32[256]{0:T(256)S(1)} %copy-done.15), kind=kLoop, calls=%fused_computation.16 | loop fusion | flops 12869632 | bytes 12870656 | tf_op jit(solution)/shard_map/convert_element_type | solution.py:105
  597.3 15.7 %convolution_bitcast_fusion.1 = f32[1,2048,4096]{2,1,0:T(8,128)} fusion(bf16[256,2048]{1,0:T(8,128)(2,1)S(1)} %copy-done.9, bf16[256,4096]{1,0:T(8,128)(2,1)} %add_convert_fusion), kind=kOutput, calls=%fused_computation.18 | convolution fusion | flops 4294967296 | bytes 36700160 | tf_op jit(solution)/shard_map/dot_general | solution.py:11
  613.0 14.3 %convolution_bitcast_fusion = f32[1,4096,2048]{2,1,0:T(8,128)} fusion(bf16[256,2048]{1,0:T(8,128)(2,1)S(1)} %maximum_select_fusion.5, f32[256,4096]{1,0:T(8,128)S(1)} %copy-done.7), kind=kOutput, calls=%fused_computation.17 | convolution fusion | flops 4304404480 | bytes 38797312 | tf_op jit(solution)/shard_map/dot_general | solution.py:11
  629.4 78.4 %fusion = f32[25136,2048]{1,0:T(8,128)} fusion(bf16[25136,256]{1,0:T(8,128)(2,1)} %fusion.10, bf16[25136,256]{1,0:T(8,128)(2,1)} %fusion.9, bf16[256,2048]{1,0:T(8,128)(2,1)S(1)} %add_select_fusion, bf16[256,2048]{1,0:T(8,128)(2,1)S(1)} %copy-done.11), kind=kOutput, calls=%fused_computation.1 | convolution fusion | flops 52769685504 | bytes 233750528 | tf_op jit(solution)/shard_map/dot_general | solution.py:11
  (161 shorter events, 71.3 us)
Async XLA Ops:
  10.0 18.0 %collective-permute-start = (bf16[256,2048]{1,0:T(8,128)(2,1)S(1)}, bf16[256,2048]{1,0:T(8,128)(2,1)S(1)}, u32[]{:S(2)}, u32[]{:S(2)}) collective-permute-start(bf16[256,2048]{1,0:T(8,128)(2,1)S(1)} %select_select_fusion), channel_id=1, source_target_pairs={{0,4},{4,0}} | collective-permute-start | bytes 3145736 | tf_op jit(solution)/shard_map/ppermute | solution.py:22
  46.1 16.7 %collective-permute-start.1 = (f32[128,2048]{1,0:T(8,128)S(1)}, f32[128,2048]{1,0:T(8,128)S(1)}, u32[]{:S(2)}, u32[]{:S(2)}) collective-permute-start(f32[128,2048]{1,0:T(8,128)S(1)} %constant_dynamic-slice_fusion.7), channel_id=1, source_target_pairs={{0,4},{4,0}} | collective-permute-start | bytes 3145736 | tf_op jit(solution)/shard_map/ppermute | solution.py:22
  65.0 2.8 collective-permute-start.2
  66.3 8.0 %collective-permute-start.3 = (bf16[128,2048]{1,0:T(8,128)(2,1)}, bf16[128,2048]{1,0:T(8,128)(2,1)S(1)}, u32[]{:S(2)}, u32[]{:S(2)}) collective-permute-start(bf16[128,2048]{1,0:T(8,128)(2,1)} %add_convert_fusion.11), channel_id=1, source_target_pairs={{0,5},{4,1}} | collective-permute-start | bytes 1572872 | tf_op jit(solution)/shard_map/ppermute | solution.py:22
  90.1 0.7 collective-permute-start.4
  91.8 1.4 collective-permute-start.5
  92.5 0.7 collective-permute-start.6
  111.5 0.7 collective-permute-start.7
  113.7 1.6 collective-permute-start.8
  114.4 0.9 collective-permute-start.9
  131.5 0.7 collective-permute-start.10
  132.5 0.7 collective-permute-start.11
  133.4 2.4 collective-permute-start.13
  134.1 3.3 collective-permute-start.12
  135.8 94.5 %collective-permute-start.14 = (bf16[256,2048]{1,0:T(8,128)(2,1)S(1)}, bf16[256,2048]{1,0:T(8,128)(2,1)}, u32[]{:S(2)}, u32[]{:S(2)}) collective-permute-start(bf16[256,2048]{1,0:T(8,128)(2,1)S(1)} %collective-permute-done.13), channel_id=1, source_target_pairs={{1,0},{5,4}} | collective-permute-start | bytes 3145736 | tf_op jit(solution)/shard_map/ppermute | solution.py:22
  297.5 3.6 collective-permute-start.15
  351.0 0.9 collective-permute-start.16
  354.0 1.2 collective-permute-start.17
  375.4 0.9 collective-permute-start.18
  376.7 1.6 collective-permute-start.19
  377.4 0.9 collective-permute-start.20
  403.5 0.9 collective-permute-start.21
  406.1 1.6 collective-permute-start.22
  406.8 0.9 collective-permute-start.23
  428.2 0.7 collective-permute-start.24
  430.0 90.0 %collective-permute-start.25 = (bf16[128,2048]{1,0:T(8,128)(2,1)}, bf16[128,2048]{1,0:T(8,128)(2,1)S(1)}, u32[]{:S(2)}, u32[]{:S(2)}) collective-permute-start(bf16[128,2048]{1,0:T(8,128)(2,1)} %add_convert_fusion.5), channel_id=1, source_target_pairs={{1,0},{5,4}} | collective-permute-start | bytes 1572872 | tf_op jit(solution)/shard_map/ppermute | solution.py:22
  431.3 95.5 %collective-permute-start.26 = (bf16[128,2048]{1,0:T(8,128)(2,1)}, bf16[128,2048]{1,0:T(8,128)(2,1)S(1)}, u32[]{:S(2)}, u32[]{:S(2)}) collective-permute-start(bf16[128,2048]{1,0:T(8,128)(2,1)} %add_convert_fusion.5), channel_id=1, source_target_pairs={{1,4},{5,0}} | collective-permute-start | bytes 1572872 | tf_op jit(solution)/shard_map/ppermute | solution.py:22
  552.0 16.7 %collective-permute-start.27 = (f32[128,2048]{1,0:T(8,128)S(1)}, f32[128,2048]{1,0:T(8,128)S(1)}, u32[]{:S(2)}, u32[]{:S(2)}) collective-permute-start(f32[128,2048]{1,0:T(8,128)S(1)} %constant_dynamic-slice_fusion), channel_id=1, source_target_pairs={{0,4},{4,0}} | collective-permute-start | bytes 3145736 | tf_op jit(solution)/shard_map/ppermute | solution.py:22
  570.1 11.1 %collective-permute-start.28 = (bf16[128,2048]{1,0:T(8,128)(2,1)S(1)}, bf16[128,2048]{1,0:T(8,128)(2,1)S(1)}, u32[]{:S(2)}, u32[]{:S(2)}) collective-permute-start(bf16[128,2048]{1,0:T(8,128)(2,1)S(1)} %add_convert_fusion.4), channel_id=1, source_target_pairs={{0,4},{4,0}} | collective-permute-start | bytes 1572872 | tf_op jit(solution)/shard_map/ppermute | solution.py:22
  582.4 13.9 %collective-permute-start.30 = (bf16[256,2048]{1,0:T(8,128)(2,1)}, bf16[256,2048]{1,0:T(8,128)(2,1)}, u32[]{:S(2)}, u32[]{:S(2)}) collective-permute-start(bf16[256,2048]{1,0:T(8,128)(2,1)} %pad_maximum_fusion.2), channel_id=1, source_target_pairs={{0,2},{4,6}} | collective-permute-start | bytes 3145736 | tf_op jit(solution)/shard_map/ppermute | solution.py:22
  594.6 32.7 %collective-permute-start.29 = (bf16[256,2048]{1,0:T(8,128)(2,1)}, bf16[256,2048]{1,0:T(8,128)(2,1)S(1)}, u32[]{:S(2)}, u32[]{:S(2)}) collective-permute-start(bf16[256,2048]{1,0:T(8,128)(2,1)} %pad_maximum_fusion.2), channel_id=1, source_target_pairs={{0,1},{4,5}} | collective-permute-start | bytes 3145736 | tf_op jit(solution)/shard_map/ppermute | solution.py:22
  596.3 31.0 %collective-permute-start.31 = (bf16[256,2048]{1,0:T(8,128)(2,1)}, bf16[256,2048]{1,0:T(8,128)(2,1)S(1)}, u32[]{:S(2)}, u32[]{:S(2)}) collective-permute-start(bf16[256,2048]{1,0:T(8,128)(2,1)} %collective-permute-done.30), channel_id=1, source_target_pairs={{2,3},{6,7}} | collective-permute-start | bytes 3145736 | tf_op jit(solution)/shard_map/ppermute | solution.py:22
  (25 other events, 361.6 us)

commit v2 on v1

v2 whole, which is shorter than its diff:
```python
import jax
import jax.numpy as jnp
from jax import lax
from jax.experimental import pallas as pl
from jax.experimental.pallas import tpu as pltpu
from jax.sharding import PartitionSpec as P

NORM_EPS = 1e-6
AXES = ('tp', 'pp')
NUM_CHUNKS = 2
ROW_GROUP = 8
TABLE_BLOCK = 528


def contract(lhs, rhs, lhs_dim, rhs_dim):
    return lax.dot_general(lhs, rhs, (((lhs_dim,), (rhs_dim,)), ((), ())), preferred_element_type=jnp.float32)


def empty_kernel(table_ref):
    pass


def head_kernel(base_ref, grad_ref, normed_ref, table_in, table_ref):
    table_ref[...] = jnp.dot(grad_ref[...], normed_ref[...], preferred_element_type=jnp.float32)


def head_rows(base, grad_logits, normed_b, table, num_steps):
    vocab_rows, model_dim = table.shape
    num_tok = normed_b.shape[0]
    return pl.pallas_call(
        head_kernel,
        out_shape=jax.ShapeDtypeStruct(table.shape, table.dtype),
        grid_spec=pltpu.PrefetchScalarGridSpec(
            num_scalar_prefetch=1,
            grid=(num_steps,),
            in_specs=[
                pl.BlockSpec((TABLE_BLOCK, num_tok), lambda i, base_ref: (base_ref[0] + i, 0)),
                pl.BlockSpec((num_tok, model_dim), lambda i, base_ref: (0, 0)),
                pl.BlockSpec(memory_space=pl.ANY),
            ],
            out_specs=pl.BlockSpec((TABLE_BLOCK, model_dim), lambda i, base_ref: (base_ref[0] + i, 0)),
        ),
        input_output_aliases={3: 0},
        compiler_params=pltpu.CompilerParams(dimension_semantics=('arbitrary',), vmem_limit_bytes=24 << 20),
        cost_estimate=pl.CostEstimate(flops=2 * num_steps * TABLE_BLOCK * model_dim * num_tok, bytes_accessed=4 * num_steps * TABLE_BLOCK * model_dim, transcendentals=0),
        name='head_rows',
    )(base, grad_logits, normed_b, table)


def add_kernel(group_ref, used_ref, pick_ref, rows_ref, table_in, table_ref, held_ref, sem):
    num_slots = group_ref.shape[0]
    part = 32 * ROW_GROUP

    def there(slot):
        return table_ref.at[pl.ds(pl.multiple_of(group_ref[slot] * ROW_GROUP, ROW_GROUP), ROW_GROUP), :]

    def here(slot):
        return held_ref.at[pl.ds(pl.multiple_of(slot * ROW_GROUP, ROW_GROUP), ROW_GROUP), :]

    def each(action):
        def step(slot, carry):
            @pl.when(used_ref[slot] == 1)
            def _():
                action(slot)
            return carry
        lax.fori_loop(0, num_slots, step, 0)

    each(lambda slot: pltpu.make_async_copy(there(slot), here(slot), sem.at[0]).start())
    each(lambda slot: pltpu.make_async_copy(there(slot), here(slot), sem.at[0]).wait())

    def add_part(index, carry):
        rows = pl.ds(pl.multiple_of(index * part, part), part)
        held_ref[rows, :] += jnp.dot(pick_ref[rows, :], rows_ref[...], preferred_element_type=jnp.float32)
        return carry

    lax.fori_loop(0, num_slots * ROW_GROUP // part, add_part, 0)
    each(lambda slot: pltpu.make_async_copy(here(slot), there(slot), sem.at[1]).start())
    each(lambda slot: pltpu.make_async_copy(here(slot), there(slot), sem.at[1]).wait())


def add_rows(group, used, pick, rows, table):
    num_slots, model_dim = rows.shape
    whole = pl.BlockSpec(memory_space=pltpu.VMEM)
    return pl.pallas_call(
        add_kernel,
        out_shape=jax.ShapeDtypeStruct(table.shape, table.dtype),
        in_specs=[pl.BlockSpec(memory_space=pltpu.SMEM), pl.BlockSpec(memory_space=pltpu.SMEM), whole, whole, pl.BlockSpec(memory_space=pl.ANY)],
        out_specs=pl.BlockSpec(memory_space=pl.ANY),
        scratch_shapes=[pltpu.VMEM((num_slots * ROW_GROUP, model_dim), jnp.float32), pltpu.SemaphoreType.DMA((2,))],
        input_output_aliases={4: 0},
        compiler_params=pltpu.CompilerParams(vmem_limit_bytes=32 << 20),
        name='add_rows',
    )(group, used, pick, rows, table)


def solution(mesh):
    pp_size = mesh.shape['pp']
    last = pp_size - 1

    def link(src_stage, dst_stage, cross):
        return [(t * pp_size + src_stage, (1 - t if cross else t) * pp_size + dst_stage) for t in range(2)]

    def send(value, src_stage, dst_stage, cross):
        return lax.ppermute(value, AXES, link(src_stage, dst_stage, cross))

    def device_fn(tokens, labels, emb_table, w_in, w_out):
        num_micro, seq_len = tokens.shape
        num_tok = num_micro * seq_len
        chunk_len = num_tok // NUM_CHUNKS
        half = chunk_len // 2
        chunks = range(NUM_CHUNKS)
        vocab_rows, model_dim = emb_table.shape
        w_one = w_in[0]
        w_two = w_out[0]
        stage_idx = lax.axis_index('pp')
        tp_idx = lax.axis_index('tp')
        is_low = tp_idx == 0
        vocab_base = tp_idx * vocab_rows
        tok_local = tokens.reshape(num_tok) - vocab_base
        lab_local = labels.reshape(num_tok) - vocab_base
        row_ids = jnp.arange(vocab_rows, dtype=jnp.int32)

        def cut(value, chunk):
            return value[chunk * chunk_len:(chunk + 1) * chunk_len]

        def mine(value):
            return lax.dynamic_slice_in_dim(value, tp_idx * half, half, 0)

        def theirs(value):
            return lax.dynamic_slice_in_dim(value, (1 - tp_idx) * half, half, 0)

        def join(own, other):
            return jnp.concatenate([jnp.where(is_low, own, other), jnp.where(is_low, other, own)], axis=0)

        def reduce_half(partial, stage):
            return mine(partial) + send(theirs(partial), stage, stage, True)

        def spread(value_half, source, far, near, rest):
            pair = join(value_half, send(value_half, source, source, True))
            middle = send(pair, source, far, False)
            others = send(pair, source, near, False) + middle + send(middle, far, rest, False)
            return jnp.where(stage_idx == source, pair, others)

        owned = (tok_local >= 0) & (tok_local < vocab_rows)
        looked_up = jnp.take(emb_table, jnp.clip(tok_local, 0, vocab_rows - 1), axis=0)
        looked_up = jnp.where(owned[:, None], looked_up, jnp.zeros_like(looked_up))
        x_act = [cut(looked_up, c) + send(cut(looked_up, c), 0, 0, True) for c in chunks]
        hidden, gate_act, y_half = [None] * NUM_CHUNKS, [None] * NUM_CHUNKS, [None] * NUM_CHUNKS

        for stage in range(pp_size):
            for c in chunks:
                hidden[c] = jnp.dot(x_act[c], w_one, preferred_element_type=jnp.float32)
                gate_act[c] = jax.nn.gelu(hidden[c]).astype(jnp.bfloat16)
                branch = reduce_half(jnp.dot(gate_act[c], w_two, preferred_element_type=jnp.float32), stage)
                y_half[c] = (mine(x_act[c]).astype(jnp.float32) + branch).astype(jnp.bfloat16)
                if stage < last:
                    arrived = join(send(y_half[c], stage, stage + 1, False), send(y_half[c], stage, stage + 1, True))
                    x_act[c] = jnp.where(stage_idx == stage + 1, arrived, x_act[c])

        y_top = jnp.concatenate([spread(y_half[c], last, 1, 2, 0) for c in chunks], axis=0)

        x_wide = y_top.astype(jnp.float32)
        inv_rms = lax.rsqrt(jnp.mean(x_wide * x_wide, axis=-1, keepdims=True) + NORM_EPS)
        normed = x_wide * inv_rms
        normed_b = normed.astype(jnp.bfloat16)
        logits = contract(emb_table, normed_b, 1, 1)
        target_hit = row_ids[:, None] == lab_local[None, :]
        local_max = jnp.max(logits, axis=0)
        local_sum = jnp.sum(jnp.exp(logits - local_max[None, :]), axis=0)
        local_target = jnp.sum(jnp.where(target_hit, logits, 0.0), axis=0)
        stats = jnp.stack([jnp.log(local_sum) + local_max, local_target])
        other = lax.ppermute(stats, 'tp', [(0, 1), (1, 0)])
        log_norm = jnp.logaddexp(stats[0], other[0])
        mean_loss = jnp.sum(log_norm - (stats[1] + other[1])) / num_tok
        grad_logits = (jnp.exp(logits - log_norm[None, :]) - target_hit.astype(jnp.float32)).astype(jnp.bfloat16)
        normed_part = contract(grad_logits, emb_table, 0, 0)
        grad_y = [None] * NUM_CHUNKS
        for c in chunks:
            grad_normed = reduce_half(cut(normed_part, c), last)
            normed_h = mine(cut(normed, c))
            grad_half = (mine(cut(inv_rms, c)) * (grad_normed - normed_h * jnp.mean(normed_h * grad_normed, axis=-1, keepdims=True))).astype(jnp.bfloat16)
            grad_y[c] = join(grad_half, send(grad_half, last, last, True))

        num_fill = (pp_size - 1) * NUM_CHUNKS
        fill_steps = pl.cdiv(pl.cdiv(vocab_rows, TABLE_BLOCK), num_fill)
        table = pl.pallas_call(empty_kernel, out_shape=jax.ShapeDtypeStruct((vocab_rows, model_dim), jnp.float32), out_specs=pl.BlockSpec(memory_space=pl.ANY), name='empty_table')()
        grad_hidden, dx_half = [jnp.zeros(hidden[0].shape, jnp.bfloat16)] * NUM_CHUNKS, [None] * NUM_CHUNKS
        for stage in range(last, -1, -1):
            for c in chunks:
                slot = (last - stage) * NUM_CHUNKS + c
                turn = slot - jnp.where(slot > (last - stage_idx) * NUM_CHUNKS, NUM_CHUNKS, 0)

                def run_stage(operands):
                    dy, wide, kept, held = operands
                    dh = jax.vjp(jax.nn.gelu, wide)[1](contract(dy, w_two, 1, 1))[0].astype(jnp.bfloat16)
                    return contract(dh, w_one, 1, 1), dh, held

                def fill_table(operands):
                    dy, wide, kept, held = operands
                    base = (turn * fill_steps).astype(jnp.int32).reshape(1)
                    return jnp.zeros(dy.shape, jnp.float32), kept, head_rows(base, grad_logits, normed_b, held, fill_steps)

                partial, grad_hidden[c], table = lax.cond(stage_idx == stage, run_stage, fill_table, (grad_y[c], hidden[c], grad_hidden[c], table))
                dx_half[c] = (mine(grad_y[c]).astype(jnp.float32) + reduce_half(partial, stage)).astype(jnp.bfloat16)
                if stage > 0:
                    arrived = join(send(dx_half[c], stage, stage - 1, False), send(dx_half[c], stage, stage - 1, True))
                    grad_y[c] = jnp.where(stage_idx == stage - 1, arrived, grad_y[c])

        dx_rows = jnp.concatenate([spread(dx_half[c], 0, 2, 1, 3) for c in chunks], axis=0)
        grad_two = contract(jnp.concatenate(gate_act, axis=0), jnp.concatenate(grad_y, axis=0), 0, 0)
        grad_one = contract(jnp.concatenate(x_act, axis=0), jnp.concatenate(grad_hidden, axis=0), 0, 0)
        slot_ids = jnp.arange(num_tok, dtype=jnp.int32)
        group = jnp.where(owned, tok_local // ROW_GROUP, -1)
        first = jnp.min(jnp.where(group[:, None] == group[None, :], slot_ids[None, :], num_tok), axis=1)
        used = (owned & (first == slot_ids)).astype(jnp.int32)
        slot_rows = (jnp.maximum(group, 0) * ROW_GROUP)[:, None] + jnp.arange(ROW_GROUP, dtype=jnp.int32)[None, :]
        pick = ((slot_rows[:, :, None] == tok_local[None, None, :]) & (used[:, None, None] == 1)).astype(jnp.bfloat16).reshape(num_tok * ROW_GROUP, num_tok)
        grad_table = add_rows(jnp.maximum(group, 0), used, pick, dx_rows, table)
        return mean_loss.reshape(1), grad_one[None], grad_two[None], grad_table

    return jax.shard_map(device_fn, mesh=mesh, in_specs=(P('dp', None), P('dp', None), P('tp', None), P('pp', None, 'tp'), P('pp', 'tp', None)), out_specs=(P('dp'), P(('dp', 'pp'), None, 'tp'), P(('dp', 'pp'), 'tp', None), P(('dp', 'tp'), None)), check_vma=False)
```

time: 716 us -> 758 us (1.059)
  Pallas kernels: 0 us -> 95.6 us
  waiting for transfers between devices: 243 us -> 160 us
  matrix products: 348 us -> 301 us
  starting transfers between devices: 44.8 us -> 85.8 us
  local copies, waits for them, and re-layouts: 16.2 us -> 33.7 us
  other arithmetic: 54 us -> 67.6 us
    dot_general x13 -> x8, matrix products: 286 us -> 173 us  [contract(): lax.dot_general(lhs, rhs, (((lhs_dim,), (rhs_dim,)), ((), ())), preferred...]
    pallas_call x0 -> x8, Pallas kernels: none -> 95.6 us  [the longest x6 80.6 us: head_rows(): pl.pallas_call(head_kernel, out_shape=jax.ShapeDtypeStruct(table.shape, t...]
    ppermute x31 -> x62, waiting for transfers between devices: 239 us -> 156 us  [send(): return lax.ppermute(value, AXES, link(src_stage, dst_stage, cross))]
    dot_general x5 -> x10, matrix products: 61.8 us -> 127 us  [the longest x8 113 us: device_fn(): jnp.dot(gate_act[c], w_two, preferred_element_type=jnp.float32)]
    ppermute x31 -> x62, starting transfers between devices: 44.5 us -> 83.6 us  [send(): return lax.ppermute(value, AXES, link(src_stage, dst_stage, cross))]
    dynamic_slice x9 -> x18, local copies, waits for them, and re-layouts: 5.66 us -> 13.3 us  [theirs(): return lax.dynamic_slice_in_dim(value, (1 - tp_idx) * half, half, 0)]
    convert_element_type x10 -> x19, other arithmetic: 18.3 us -> 20.3 us  [the longest x8 12.2 us: device_fn(): (mine(grad_y[c]).astype(jnp.float32) + reduce_half(partial, stage)).astyp...]
  transfers between devices with their start and end apart: 32 -> 63, of which waited for: 9 -> 10; matrix products, arithmetic and copies ran while one was open for 6% -> 33% of each run, Pallas kernels for 0% -> 11%
where the time goes in v2:
time: 758 us; the launch traced here: 749 us
  matrix products  301 us (40%)
  waiting for transfers between devices  160 us (21%)
  Pallas kernels  95.6 us (13%)
  starting transfers between devices  85.8 us (11%)
  other arithmetic  67.6 us (9%)
  local copies, waits for them, and re-layouts  33.7 us (4%)
    dot_general x8, matrix products, contract(): lax.dot_general(lhs, rhs, (((lhs_dim,), (rhs_dim,)), ((), ())), preferred...  173 us
    ppermute x62, waiting for transfers between devices, send(): return lax.ppermute(value, AXES, link(src_stage, dst_stage, cross))  156 us
    dot_general x8, matrix products, device_fn(): jnp.dot(gate_act[c], w_two, preferred_element_type=jnp.float32)  113 us
    ppermute x62, starting transfers between devices, send(): return lax.ppermute(value, AXES, link(src_stage, dst_stage, cross))  83.6 us
    pallas_call x6, Pallas kernels, head_rows(): pl.pallas_call(head_kernel, out_shape=jax.ShapeDtypeStruct(table.shape, t...  80.6 us
  transfers between devices with their start and end apart: 63, of which 10 were waited for; matrix products, arithmetic and copies ran while one was open for 33% of the time, Pallas kernels for 11%

profile of v2, /device:TPU:0, one launch (start us, length us, event | category | flops | bytes accessed | tf_op | source)
XLA Modules:
  0.0 749.2 jit_solution(15018053134640305694)
XLA Ops:
  29.4 15.6 %fusion.143 = f32[128,2048]{1,0:T(8,128)S(1)} fusion(bf16[1,4096,2048]{2,1,0:T(8,128)(2,1)} %param.25, bf16[128,2048]{1,0:T(8,128)(2,1)S(1)} %get-tuple-element.495, bf16[1,2048,4096]{2,1,0:T(8,128)(2,1)} %param.24), kind=kOutput, calls=%fused_computation.172 | convolution fusion | flops 4299685888 | bytes 35127296 | tf_op jit(solution)/shard_map/dot_general | solution.py:154
  49.9 15.6 %fusion.137 = f32[128,2048]{1,0:T(8,128)S(1)} fusion(bf16[1,4096,2048]{2,1,0:T(8,128)(2,1)} %param.25, bf16[128,2048]{1,0:T(8,128)(2,1)S(1)} %get-tuple-element.496, bf16[1,2048,4096]{2,1,0:T(8,128)(2,1)} %param.24), kind=kOutput, calls=%fused_computation.169 | convolution fusion | flops 4299685888 | bytes 35127296 | tf_op jit(solution)/shard_map/dot_general | solution.py:154
  82.8 15.6 %fusion.141 = f32[128,2048]{1,0:T(8,128)S(1)} fusion(bf16[1,4096,2048]{2,1,0:T(8,128)(2,1)} %param.25, bf16[128,2048]{1,0:T(8,128)(2,1)S(1)} %maximum_select_fusion, bf16[1,2048,4096]{2,1,0:T(8,128)(2,1)} %param.24), kind=kOutput, calls=%fused_computation.171 | convolution fusion | flops 4299685888 | bytes 35127296 | tf_op jit(solution)/shard_map/dot_general | solution.py:154
  101.5 16.6 %fusion.135 = f32[128,2048]{1,0:T(8,128)} fusion(bf16[1,4096,2048]{2,1,0:T(8,128)(2,1)} %param.25, bf16[128,2048]{1,0:T(8,128)(2,1)S(1)} %maximum_select_fusion.3, bf16[1,2048,4096]{2,1,0:T(8,128)(2,1)} %param.24), kind=kOutput, calls=%fused_computation.168 | convolution fusion | flops 4299685888 | bytes 35127296 | tf_op jit(solution)/shard_map/dot_general | solution.py:154
  126.2 15.6 %fusion.139 = f32[128,2048]{1,0:T(8,128)S(1)} fusion(bf16[1,4096,2048]{2,1,0:T(8,128)(2,1)} %param.25, bf16[128,2048]{1,0:T(8,128)(2,1)S(1)} %maximum_select_fusion.1, bf16[1,2048,4096]{2,1,0:T(8,128)(2,1)} %param.24), kind=kOutput, calls=%fused_computation.170 | convolution fusion | flops 4299685888 | bytes 35127296 | tf_op jit(solution)/shard_map/dot_general | solution.py:154
  144.7 16.6 %fusion.133 = f32[128,2048]{1,0:T(8,128)} fusion(bf16[1,4096,2048]{2,1,0:T(8,128)(2,1)} %param.25, bf16[128,2048]{1,0:T(8,128)(2,1)S(1)} %maximum_select_fusion.4, bf16[1,2048,4096]{2,1,0:T(8,128)(2,1)} %param.24), kind=kOutput, calls=%fused_computation.167 | convolution fusion | flops 4299685888 | bytes 35127296 | tf_op jit(solution)/shard_map/dot_general | solution.py:154
  211.0 32.4 %collective-permute-done.14 = bf16[128,2048]{1,0:T(8,128)(2,1)} collective-permute-done((bf16[128,2048]{1,0:T(8,128)(2,1)S(1)}, bf16[128,2048]{1,0:T(8,128)(2,1)}, u32[]{:S(2)}, u32[]{:S(2)}) %collective-permute-start.14) | collective-permute-done | bytes 524320 | tf_op jit(solution)/shard_map/ppermute | solution.py:104
  252.6 49.6 %fusion.262 = (f32[256]{0:T(256)S(1)}, f32[256,25136]{0,1:T(8,128)}) fusion(bf16[256,2048]{1,0:T(8,128)(2,1)S(1)} %get-tuple-element.494, bf16[25136,2048]{1,0:T(8,128)(2,1)} %param.23), kind=kOutput, calls=%fused_computation.397 | convolution fusion | flops 26363441152 | bytes 129745920 | tf_op jit(solution)/shard_map/dot_general | solution.py:16
  302.2 13.2 %fusion.57 = (f32[256]{0:T(256)S(1)}, f32[256]{0:T(256)S(1)}) fusion(f32[256,25136]{0,1:T(8,128)} %get-tuple-element.547, f32[256]{0:T(256)S(1)} %get-tuple-element.546, s32[256]{0:T(256)S(1)} %sub.197), kind=kLoop, calls=%fused_computation.77 | loop fusion | flops 32173568 | bytes 25743360 | tf_op jit(solution)/shard_map/reduce_sum | solution.py:169
  330.2 41.3 %fusion.271 = f32[256,2048]{1,0:T(8,128)} fusion(bf16[25136,256]{1,0:T(8,128)(2,1)} %fusion.61, bf16[25136,2048]{1,0:T(8,128)(2,1)} %param.23), kind=kOutput, calls=%fused_computation.406 | convolution fusion | flops 26357006336 | bytes 117923840 | tf_op jit(solution)/shard_map/dot_general | solution.py:16
  378.9 14.7 %conditional.8 = (f32[128,2048]{1,0:T(8,128)S(1)}, bf16[128,4096]{1,0:T(8,128)(2,1)}, f32[25136,2048]{1,0:T(8,128)}) conditional(s32[]{:T(128)} %convert_element_type.216, (s32[]{:T(128)}, bf16[25136,256]{1,0:T(8,128)(2,1)}, bf16[256,2048]{1,0:T(8,128)(2,1)S(1)}, f32[25136,2048]{1,0:T(8,128)}) %tuple.97, (bf16[128,2048]{1,0:T(8,128)(2,1)S(1)}, ...), branch_computations={%region_6.7_spmd, %region_7.8_spmd} | conditional | flops 4429185024 | bytes 39321624 | solution.py:203
  378.9 13.5 %head_rows.19 = f32[25136,2048]{1,0:T(8,128)} custom-call(s32[1]{0:T(128)} %bitcast.base_ref, bf16[25136,256]{1,0:T(8,128)(2,1)} %get-tuple-element.352.grad_ref, bf16[256,2048]{1,0:T(8,128)(2,1)S(1)} %get-tuple-element.353.normed_ref, f32[25136,2048]{1,0:T(8,128)} %get-tuple-element.354.table_in), custom_call_target="tpu_custom_call", output_to_operand_aliasing={{}: (3, {})} | custom-call | flops 4429185024 | bytes 34603008 | tf_op jit(solution)/shard_map/cond/branch_0_fun/head_rows/pallas_call | solution.py:30
  397.7 14.9 %conditional.9 = (f32[128,2048]{1,0:T(8,128)S(1)}, bf16[128,4096]{1,0:T(8,128)(2,1)}, f32[25136,2048]{1,0:T(8,128)}) conditional(s32[]{:T(128)} %convert_element_type.216, (s32[]{:T(128)}, bf16[25136,256]{1,0:T(8,128)(2,1)}, bf16[256,2048]{1,0:T(8,128)(2,1)S(1)}, f32[25136,2048]{1,0:T(8,128)}) %tuple.99, (bf16[128,2048]{1,0:T(8,128)(2,1)}, ...), branch_computations={%region_9.10_spmd, %region_10.11_spmd} | conditional | flops 4429185024 | bytes 39321624 | solution.py:203
  397.7 13.5 %head_rows.20 = f32[25136,2048]{1,0:T(8,128)} custom-call(s32[1]{0:T(128)} %bitcast.1.base_ref, bf16[25136,256]{1,0:T(8,128)(2,1)} %get-tuple-element.361.grad_ref, bf16[256,2048]{1,0:T(8,128)(2,1)S(1)} %get-tuple-element.362.normed_ref, f32[25136,2048]{1,0:T(8,128)} %get-tuple-element.363.table_in), custom_call_target="tpu_custom_call", output_to_operand_aliasing={{}: (3, {})} | custom-call | flops 4429185024 | bytes 34603008 | tf_op jit(solution)/shard_map/cond/branch_0_fun/head_rows/pallas_call | solution.py:30
  423.4 14.0 %conditional.10 = (f32[128,2048]{1,0:T(8,128)S(1)}, bf16[128,4096]{1,0:T(8,128)(2,1)}, f32[25136,2048]{1,0:T(8,128)}) conditional(s32[]{:T(128)} %convert_element_type.215, (s32[]{:T(128)}, bf16[25136,256]{1,0:T(8,128)(2,1)}, bf16[256,2048]{1,0:T(8,128)(2,1)S(1)}, f32[25136,2048]{1,0:T(8,128)}, bf16[128,4096]{1,0:T(8,128)(2,1)}) %tuple.101, ...), branch_computations={%region_11.12_spmd, %region_12.13_spmd} | conditional | flops 4429185024 | bytes 39321624 | solution.py:203
  423.4 13.5 %head_rows.21 = f32[25136,2048]{1,0:T(8,128)} custom-call(s32[1]{0:T(128)} %bitcast.2.base_ref, bf16[25136,256]{1,0:T(8,128)(2,1)} %get-tuple-element.371.grad_ref, bf16[256,2048]{1,0:T(8,128)(2,1)S(1)} %get-tuple-element.372.normed_ref, f32[25136,2048]{1,0:T(8,128)} %get-tuple-element.373.table_in), custom_call_target="tpu_custom_call", output_to_operand_aliasing={{}: (3, {})} | custom-call | flops 4429185024 | bytes 34603008 | tf_op jit(solution)/shard_map/cond/branch_0_fun/head_rows/pallas_call | solution.py:30
  441.8 13.8 %conditional.11 = (f32[128,2048]{1,0:T(8,128)S(1)}, bf16[128,4096]{1,0:T(8,128)(2,1)}, f32[25136,2048]{1,0:T(8,128)}) conditional(s32[]{:T(128)} %convert_element_type.215, (s32[]{:T(128)}, bf16[25136,256]{1,0:T(8,128)(2,1)}, bf16[256,2048]{1,0:T(8,128)(2,1)S(1)}, f32[25136,2048]{1,0:T(8,128)}, bf16[128,4096]{1,0:T(8,128)(2,1)}) %tuple.103, ...), branch_computations={%region_13.14_spmd, %region_14.15_spmd} | conditional | flops 4429185024 | bytes 39321624 | solution.py:203
  441.8 13.5 %head_rows.22 = f32[25136,2048]{1,0:T(8,128)} custom-call(s32[1]{0:T(128)} %bitcast.3.base_ref, bf16[25136,256]{1,0:T(8,128)(2,1)} %get-tuple-element.381.grad_ref, bf16[256,2048]{1,0:T(8,128)(2,1)S(1)} %get-tuple-element.382.normed_ref, f32[25136,2048]{1,0:T(8,128)} %get-tuple-element.383.table_in), custom_call_target="tpu_custom_call", output_to_operand_aliasing={{}: (3, {})} | custom-call | flops 4429185024 | bytes 34603008 | tf_op jit(solution)/shard_map/cond/branch_0_fun/head_rows/pallas_call | solution.py:30
  467.3 13.8 %conditional.12 = (f32[128,2048]{1,0:T(8,128)S(1)}, bf16[128,4096]{1,0:T(8,128)(2,1)}, f32[25136,2048]{1,0:T(8,128)}) conditional(s32[]{:T(128)} %convert_element_type.214, (s32[]{:T(128)}, bf16[25136,256]{1,0:T(8,128)(2,1)}, bf16[256,2048]{1,0:T(8,128)(2,1)S(1)}, f32[25136,2048]{1,0:T(8,128)}, bf16[128,4096]{1,0:T(8,128)(2,1)}) %tuple.105, ...), branch_computations={%region_15.16_spmd, %region_16.17_spmd} | conditional | flops 4429185024 | bytes 39321624 | solution.py:203
  467.3 13.5 %head_rows.23 = f32[25136,2048]{1,0:T(8,128)} custom-call(s32[1]{0:T(128)} %bitcast.4.base_ref, bf16[25136,256]{1,0:T(8,128)(2,1)} %get-tuple-element.391.grad_ref, bf16[256,2048]{1,0:T(8,128)(2,1)S(1)} %get-tuple-element.392.normed_ref, f32[25136,2048]{1,0:T(8,128)} %get-tuple-element.393.table_in), custom_call_target="tpu_custom_call", output_to_operand_aliasing={{}: (3, {})} | custom-call | flops 4429185024 | bytes 34603008 | tf_op jit(solution)/shard_map/cond/branch_0_fun/head_rows/pallas_call | solution.py:30
  485.4 13.5 %conditional.13 = (f32[128,2048]{1,0:T(8,128)S(1)}, bf16[128,4096]{1,0:T(8,128)(2,1)}, f32[25136,2048]{1,0:T(8,128)}) conditional(s32[]{:T(128)} %convert_element_type.214, (s32[]{:T(128)}, bf16[25136,256]{1,0:T(8,128)(2,1)}, bf16[256,2048]{1,0:T(8,128)(2,1)S(1)}, f32[25136,2048]{1,0:T(8,128)}, bf16[128,4096]{1,0:T(8,128)(2,1)}) %tuple.107, ...), branch_computations={%region_17.18_spmd, %region_18.19_spmd} | conditional | flops 4429185024 | bytes 39321624 | solution.py:203
  485.4 13.0 %head_rows.24 = f32[25136,2048]{1,0:T(8,128)} custom-call(s32[1]{0:T(128)} %bitcast.5.base_ref, bf16[25136,256]{1,0:T(8,128)(2,1)} %get-tuple-element.401.grad_ref, bf16[256,2048]{1,0:T(8,128)(2,1)S(1)} %get-tuple-element.402.normed_ref, f32[25136,2048]{1,0:T(8,128)} %get-tuple-element.403.table_in), custom_call_target="tpu_custom_call", output_to_operand_aliasing={{}: (3, {})} | custom-call | flops 4429185024 | bytes 34603008 | tf_op jit(solution)/shard_map/cond/branch_0_fun/head_rows/pallas_call | solution.py:30
  511.6 92.8 %collective-permute-done.48 = bf16[64,2048]{1,0:T(8,128)(2,1)S(1)} collective-permute-done((bf16[64,2048]{1,0:T(8,128)(2,1)S(1)}, bf16[64,2048]{1,0:T(8,128)(2,1)S(1)}, u32[]{:S(2)}, u32[]{:S(2)}) %collective-permute-start.48) | collective-permute-done | bytes 262176 | tf_op jit(solution)/shard_map/ppermute | solution.py:104
  610.7 25.7 %conditional.14 = (f32[128,2048]{1,0:T(8,128)S(1)}, bf16[128,4096]{1,0:T(8,128)(2,1)}, f32[25136,2048]{1,0:T(8,128)}) conditional(s32[]{:T(128)} %convert_element_type.211, (s32[]{:T(128)}, bf16[25136,256]{1,0:T(8,128)(2,1)}, bf16[256,2048]{1,0:T(8,128)(2,1)S(1)}, f32[25136,2048]{1,0:T(8,128)}, bf16[128,4096]{1,0:T(8,128)(2,1)}) %tuple.109, ...), branch_computations={%region_19.20_spmd, %region_20.21_spmd} | conditional | flops 4429185024 | bytes 39321624 | solution.py:203
  610.8 13.8 %fusion.48 = bf16[128,4096]{1,0:T(8,128)(2,1)} fusion(f32[128,4096]{1,0:T(8,128)} %get-tuple-element.416, bf16[128,2048]{1,0:T(8,128)(2,1)} %get-tuple-element.414, bf16[4096,2048]{1,0:T(8,128)(2,1)} %get-tuple-element.415), kind=kOutput, calls=%fused_computation.63 | convolution fusion | flops 2157969408 | bytes 20447232 | tf_op jit(solution)/shard_map/cond/branch_1_fun/dot_general | solution.py:16
  624.6 11.8 %fusion.269 = f32[128,2048]{1,0:T(8,128)S(1)} fusion(bf16[128,4096]{1,0:T(8,128)(2,1)} %fusion.48, bf16[2048,4096]{1,0:T(8,128)(2,1)} %get-tuple-element.417), kind=kOutput, calls=%fused_computation.404 | convolution fusion | flops 2147483648 | bytes 18874368 | tf_op jit(solution)/shard_map/cond/branch_1_fun/dot_general | solution.py:16
  642.0 25.7 %conditional.15 = (f32[128,2048]{1,0:T(8,128)S(1)}, bf16[128,4096]{1,0:T(8,128)(2,1)}, f32[25136,2048]{1,0:T(8,128)}) conditional(s32[]{:T(128)} %convert_element_type.211, (s32[]{:T(128)}, bf16[25136,256]{1,0:T(8,128)(2,1)}, bf16[256,2048]{1,0:T(8,128)(2,1)S(1)}, f32[25136,2048]{1,0:T(8,128)}, bf16[128,4096]{1,0:T(8,128)(2,1)}) %tuple.111, ...), branch_computations={%region_21.22_spmd, %region_22.23_spmd} | conditional | flops 4429185024 | bytes 39321624 | solution.py:203
  642.2 13.8 %fusion.55 = bf16[128,4096]{1,0:T(8,128)(2,1)} fusion(f32[128,4096]{1,0:T(8,128)} %get-tuple-element.426, bf16[128,2048]{1,0:T(8,128)(2,1)} %get-tuple-element.424, bf16[4096,2048]{1,0:T(8,128)(2,1)} %get-tuple-element.425), kind=kOutput, calls=%fused_computation.72 | convolution fusion | flops 2157969408 | bytes 20447232 | tf_op jit(solution)/shard_map/cond/branch_1_fun/dot_general | solution.py:16
  656.0 11.8 %fusion.270 = f32[128,2048]{1,0:T(8,128)S(1)} fusion(bf16[128,4096]{1,0:T(8,128)(2,1)} %fusion.55, bf16[2048,4096]{1,0:T(8,128)(2,1)} %get-tuple-element.427), kind=kOutput, calls=%fused_computation.405 | convolution fusion | flops 2147483648 | bytes 18874368 | tf_op jit(solution)/shard_map/cond/branch_1_fun/dot_general | solution.py:16
  696.6 15.3 %convolution_bitcast_fusion = f32[1,4096,2048]{2,1,0:T(8,128)} fusion(bf16[128,4096]{1,0:T(8,128)(2,1)S(1)} %copy-done.5, bf16[128,4096]{1,0:T(8,128)(2,1)S(1)} %copy-done.3, bf16[128,2048]{1,0:T(8,128)(2,1)} %maximum_select_fusion.11, bf16[128,2048]{1,0:T(8,128)(2,1)} %maximum_select_fusion.10), kind=kOutput, calls=%fused_computation.83 | convolution fusion | flops 4301258752 | bytes 36700160 | tf_op jit(solution)/shard_map/dot_general | solution.py:16
  714.2 15.7 %convolution_bitcast_fusion.1 = f32[1,2048,4096]{2,1,0:T(8,128)} fusion(bf16[128,4096]{1,0:T(8,128)(2,1)} %get-tuple-element.477, bf16[128,4096]{1,0:T(8,128)(2,1)} %get-tuple-element.473, bf16[128,2048]{1,0:T(8,128)(2,1)S(1)} %copy-done.17, bf16[128,2048]{1,0:T(8,128)(2,1)S(1)} %copy-done.15), kind=kOutput, calls=%fused_computation.84 | convolution fusion | flops 4301258752 | bytes 36700160 | tf_op jit(solution)/shard_map/dot_general | solution.py:16
  732.8 15.0 %add_rows.1 = f32[25136,2048]{1,0:T(8,128)} custom-call(s32[256]{0:T(256)S(1)} %broadcast_maximum_fusion.group_ref, s32[256]{0:T(256)S(1)} %get-tuple-element.484.used_ref, bf16[2048,256]{1,0:T(8,128)(2,1)S(1)} %and_convert_fusion.pick_ref, bf16[256,2048]{1,0:T(8,128)(2,1)S(1)} %pad_maximum_fusion.1.rows_ref, ...), custom_call_target="tpu_custom_call", output_to_operand_aliasing={{}: (4, {})} | custom-call | tf_op jit(solution)/shard_map/add_rows/pallas_call | solution.py:84
  (352 shorter events, 240.4 us)
Async XLA Ops:
  45.8 22.5 %collective-permute-start.1 = (f32[64,2048]{1,0:T(8,128)}, f32[64,2048]{1,0:T(8,128)}, u32[]{:S(2)}, u32[]{:S(2)}) collective-permute-start(f32[64,2048]{1,0:T(8,128)} %constant_dynamic-slice_fusion.17), channel_id=1, source_target_pairs={{0,4},{4,0}} | collective-permute-start | bytes 1572872 | tf_op jit(solution)/shard_map/ppermute | solution.py:104
  69.5 13.1 %collective-permute-start.2 = (bf16[64,2048]{1,0:T(8,128)(2,1)S(1)}, bf16[64,2048]{1,0:T(8,128)(2,1)S(1)}, u32[]{:S(2)}, u32[]{:S(2)}) collective-permute-start(bf16[64,2048]{1,0:T(8,128)(2,1)S(1)} %add_convert_fusion.15), channel_id=1, source_target_pairs={{0,1},{4,5}} | collective-permute-start | bytes 786440 | tf_op jit(solution)/shard_map/ppermute | solution.py:104
  79.3 21.0 %collective-permute-start.17 = (bf16[64,2048]{1,0:T(8,128)(2,1)}, bf16[64,2048]{1,0:T(8,128)(2,1)S(1)}, u32[]{:S(2)}, u32[]{:S(2)}) collective-permute-start(bf16[64,2048]{1,0:T(8,128)(2,1)} %add_convert_fusion.11), channel_id=1, source_target_pairs={{0,1},{4,5}} | collective-permute-start | bytes 786440 | tf_op jit(solution)/shard_map/ppermute | solution.py:104
  80.6 19.7 %collective-permute-start.18 = (bf16[64,2048]{1,0:T(8,128)(2,1)}, bf16[64,2048]{1,0:T(8,128)(2,1)}, u32[]{:S(2)}, u32[]{:S(2)}) collective-permute-start(bf16[64,2048]{1,0:T(8,128)(2,1)} %add_convert_fusion.11), channel_id=1, source_target_pairs={{0,5},{4,1}} | collective-permute-start | bytes 786440 | tf_op jit(solution)/shard_map/ppermute | solution.py:104
  99.2 21.4 %collective-permute-start.4 = (f32[64,2048]{1,0:T(8,128)}, f32[64,2048]{1,0:T(8,128)S(1)}, u32[]{:S(2)}, u32[]{:S(2)}) collective-permute-start(f32[64,2048]{1,0:T(8,128)} %constant_dynamic-slice_fusion.15), channel_id=1, source_target_pairs={{1,5},{5,1}} | collective-permute-start | bytes 1572872 | tf_op jit(solution)/shard_map/ppermute | solution.py:104
  124.0 19.6 %collective-permute-start.20 = (bf16[64,2048]{1,0:T(8,128)(2,1)}, bf16[64,2048]{1,0:T(8,128)(2,1)S(1)}, u32[]{:S(2)}, u32[]{:S(2)}) collective-permute-start(bf16[64,2048]{1,0:T(8,128)(2,1)} %add_convert_fusion.10), channel_id=1, source_target_pairs={{1,2},{5,6}} | collective-permute-start | bytes 786440 | tf_op jit(solution)/shard_map/ppermute | solution.py:104
  124.6 18.9 %collective-permute-start.21 = (bf16[64,2048]{1,0:T(8,128)(2,1)}, bf16[64,2048]{1,0:T(8,128)(2,1)}, u32[]{:S(2)}, u32[]{:S(2)}) collective-permute-start(bf16[64,2048]{1,0:T(8,128)(2,1)} %add_convert_fusion.10), channel_id=1, source_target_pairs={{1,6},{5,2}} | collective-permute-start | bytes 786440 | tf_op jit(solution)/shard_map/ppermute | solution.py:104
  142.6 21.2 %collective-permute-start.7 = (f32[64,2048]{1,0:T(8,128)}, f32[64,2048]{1,0:T(8,128)S(1)}, u32[]{:S(2)}, u32[]{:S(2)}) collective-permute-start(f32[64,2048]{1,0:T(8,128)} %constant_dynamic-slice_fusion.13), channel_id=1, source_target_pairs={{2,6},{6,2}} | collective-permute-start | bytes 1572872 | tf_op jit(solution)/shard_map/ppermute | solution.py:104
  166.4 21.3 %collective-permute-start.23 = (bf16[64,2048]{1,0:T(8,128)(2,1)S(1)}, bf16[64,2048]{1,0:T(8,128)(2,1)S(1)}, u32[]{:S(2)}, u32[]{:S(2)}) collective-permute-start(bf16[64,2048]{1,0:T(8,128)(2,1)S(1)} %add_convert_fusion.9), channel_id=1, source_target_pairs={{2,3},{6,7}} | collective-permute-start | bytes 786440 | tf_op jit(solution)/shard_map/ppermute | solution.py:104
  167.1 20.6 %collective-permute-start.24 = (bf16[64,2048]{1,0:T(8,128)(2,1)S(1)}, bf16[64,2048]{1,0:T(8,128)(2,1)S(1)}, u32[]{:S(2)}, u32[]{:S(2)}) collective-permute-start(bf16[64,2048]{1,0:T(8,128)(2,1)S(1)} %add_convert_fusion.9), channel_id=1, source_target_pairs={{2,7},{6,3}} | collective-permute-start | bytes 786440 | tf_op jit(solution)/shard_map/ppermute | solution.py:104
  187.0 14.8 %collective-permute-start.10 = (f32[64,2048]{1,0:T(8,128)S(1)}, f32[64,2048]{1,0:T(8,128)S(1)}, u32[]{:S(2)}, u32[]{:S(2)}) collective-permute-start(f32[64,2048]{1,0:T(8,128)S(1)} %constant_dynamic-slice_fusion.12), channel_id=1, source_target_pairs={{3,7},{7,3}} | collective-permute-start | bytes 1572872 | tf_op jit(solution)/shard_map/ppermute | solution.py:104
  206.5 37.0 %collective-permute-start.14 = (bf16[128,2048]{1,0:T(8,128)(2,1)S(1)}, bf16[128,2048]{1,0:T(8,128)(2,1)}, u32[]{:S(2)}, u32[]{:S(2)}) collective-permute-start(bf16[128,2048]{1,0:T(8,128)(2,1)S(1)} %collective-permute-done.13), channel_id=1, source_target_pairs={{1,0},{5,4}} | collective-permute-start | bytes 1572872 | tf_op jit(solution)/shard_map/ppermute | solution.py:104
  207.8 37.3 %collective-permute-start.27 = (bf16[128,2048]{1,0:T(8,128)(2,1)S(1)}, bf16[128,2048]{1,0:T(8,128)(2,1)}, u32[]{:S(2)}, u32[]{:S(2)}) collective-permute-start(bf16[128,2048]{1,0:T(8,128)(2,1)S(1)} %pad_maximum_fusion.5), channel_id=1, source_target_pairs={{3,2},{7,6}} | collective-permute-start | bytes 1572872 | tf_op jit(solution)/shard_map/ppermute | solution.py:104
  209.2 39.9 %collective-permute-start.29 = (bf16[128,2048]{1,0:T(8,128)(2,1)S(1)}, bf16[128,2048]{1,0:T(8,128)(2,1)}, u32[]{:S(2)}, u32[]{:S(2)}) collective-permute-start(bf16[128,2048]{1,0:T(8,128)(2,1)S(1)} %collective-permute-done.28), channel_id=1, source_target_pairs={{1,0},{5,4}} | collective-permute-start | bytes 1572872 | tf_op jit(solution)/shard_map/ppermute | solution.py:104
  376.6 19.2 %collective-permute-start.34 = (bf16[64,2048]{1,0:T(8,128)(2,1)S(1)}, bf16[64,2048]{1,0:T(8,128)(2,1)}, u32[]{:S(2)}, u32[]{:S(2)}) collective-permute-start(bf16[64,2048]{1,0:T(8,128)(2,1)S(1)} %multiply_convert_fusion), channel_id=1, source_target_pairs={{3,7},{7,3}} | collective-permute-start | bytes 786440 | tf_op jit(solution)/shard_map/ppermute | solution.py:104
  394.4 20.6 %collective-permute-start.35 = (f32[64,2048]{1,0:T(8,128)}, f32[64,2048]{1,0:T(8,128)}, u32[]{:S(2)}, u32[]{:S(2)}) collective-permute-start(f32[64,2048]{1,0:T(8,128)} %constant_dynamic-slice_fusion.1), channel_id=1, source_target_pairs={{3,7},{7,3}} | collective-permute-start | bytes 1572872 | tf_op jit(solution)/shard_map/ppermute | solution.py:104
  419.7 20.1 %collective-permute-start.39 = (bf16[64,2048]{1,0:T(8,128)(2,1)}, bf16[64,2048]{1,0:T(8,128)(2,1)}, u32[]{:S(2)}, u32[]{:S(2)}) collective-permute-start(bf16[64,2048]{1,0:T(8,128)(2,1)} %add_convert_fusion.6), channel_id=1, source_target_pairs={{3,2},{7,6}} | collective-permute-start | bytes 786440 | tf_op jit(solution)/shard_map/ppermute | solution.py:104
  421.1 18.8 %collective-permute-start.40 = (bf16[64,2048]{1,0:T(8,128)(2,1)}, bf16[64,2048]{1,0:T(8,128)(2,1)}, u32[]{:S(2)}, u32[]{:S(2)}) collective-permute-start(bf16[64,2048]{1,0:T(8,128)(2,1)} %add_convert_fusion.6), channel_id=1, source_target_pairs={{3,6},{7,2}} | collective-permute-start | bytes 786440 | tf_op jit(solution)/shard_map/ppermute | solution.py:104
  438.3 21.3 %collective-permute-start.41 = (f32[64,2048]{1,0:T(8,128)}, f32[64,2048]{1,0:T(8,128)}, u32[]{:S(2)}, u32[]{:S(2)}) collective-permute-start(f32[64,2048]{1,0:T(8,128)} %constant_dynamic-slice_fusion.3), channel_id=1, source_target_pairs={{2,6},{6,2}} | collective-permute-start | bytes 1572872 | tf_op jit(solution)/shard_map/ppermute | solution.py:104
  464.2 19.2 %collective-permute-start.45 = (bf16[64,2048]{1,0:T(8,128)(2,1)}, bf16[64,2048]{1,0:T(8,128)(2,1)S(1)}, u32[]{:S(2)}, u32[]{:S(2)}) collective-permute-start(bf16[64,2048]{1,0:T(8,128)(2,1)} %add_convert_fusion.4), channel_id=1, source_target_pairs={{2,1},{6,5}} | collective-permute-start | bytes 786440 | tf_op jit(solution)/shard_map/ppermute | solution.py:104
  464.9 18.6 %collective-permute-start.46 = (bf16[64,2048]{1,0:T(8,128)(2,1)}, bf16[64,2048]{1,0:T(8,128)(2,1)}, u32[]{:S(2)}, u32[]{:S(2)}) collective-permute-start(bf16[64,2048]{1,0:T(8,128)(2,1)} %add_convert_fusion.4), channel_id=1, source_target_pairs={{2,5},{6,1}} | collective-permute-start | bytes 786440 | tf_op jit(solution)/shard_map/ppermute | solution.py:104
  482.0 21.1 %collective-permute-start.47 = (f32[64,2048]{1,0:T(8,128)}, f32[64,2048]{1,0:T(8,128)}, u32[]{:S(2)}, u32[]{:S(2)}) collective-permute-start(f32[64,2048]{1,0:T(8,128)} %constant_dynamic-slice_fusion.11), channel_id=1, source_target_pairs={{1,5},{5,1}} | collective-permute-start | bytes 1572872 | tf_op jit(solution)/shard_map/ppermute | solution.py:104
  504.3 100.1 %collective-permute-start.48 = (bf16[64,2048]{1,0:T(8,128)(2,1)S(1)}, bf16[64,2048]{1,0:T(8,128)(2,1)S(1)}, u32[]{:S(2)}, u32[]{:S(2)}) collective-permute-start(bf16[64,2048]{1,0:T(8,128)(2,1)S(1)} %add_convert_fusion.3), channel_id=1, source_target_pairs={{1,0},{5,4}} | collective-permute-start | bytes 786440 | tf_op jit(solution)/shard_map/ppermute | solution.py:104
  505.6 104.1 %collective-permute-start.49 = (bf16[64,2048]{1,0:T(8,128)(2,1)S(1)}, bf16[64,2048]{1,0:T(8,128)(2,1)S(1)}, u32[]{:S(2)}, u32[]{:S(2)}) collective-permute-start(bf16[64,2048]{1,0:T(8,128)(2,1)S(1)} %add_convert_fusion.3), channel_id=1, source_target_pairs={{1,4},{5,0}} | collective-permute-start | bytes 786440 | tf_op jit(solution)/shard_map/ppermute | solution.py:104
  509.0 131.1 %collective-permute-start.51 = (bf16[64,2048]{1,0:T(8,128)(2,1)}, bf16[64,2048]{1,0:T(8,128)(2,1)S(1)}, u32[]{:S(2)}, u32[]{:S(2)}) collective-permute-start(bf16[64,2048]{1,0:T(8,128)(2,1)} %add_convert_fusion.2), channel_id=1, source_target_pairs={{1,0},{5,4}} | collective-permute-start | bytes 786440 | tf_op jit(solution)/shard_map/ppermute | solution.py:104
  510.3 129.8 %collective-permute-start.52 = (bf16[64,2048]{1,0:T(8,128)(2,1)}, bf16[64,2048]{1,0:T(8,128)(2,1)}, u32[]{:S(2)}, u32[]{:S(2)}) collective-permute-start(bf16[64,2048]{1,0:T(8,128)(2,1)} %add_convert_fusion.2), channel_id=1, source_target_pairs={{1,4},{5,0}} | collective-permute-start | bytes 786440 | tf_op jit(solution)/shard_map/ppermute | solution.py:104
  637.3 34.5 %collective-permute-start.53 = (f32[64,2048]{1,0:T(8,128)}, f32[64,2048]{1,0:T(8,128)}, u32[]{:S(2)}, u32[]{:S(2)}) collective-permute-start(f32[64,2048]{1,0:T(8,128)} %constant_dynamic-slice_fusion.14), channel_id=1, source_target_pairs={{0,4},{4,0}} | collective-permute-start | bytes 1572872 | tf_op jit(solution)/shard_map/ppermute | solution.py:104
  691.0 22.2 %collective-permute-start.61 = (bf16[128,2048]{1,0:T(8,128)(2,1)}, bf16[128,2048]{1,0:T(8,128)(2,1)}, u32[]{:S(2)}, u32[]{:S(2)}) collective-permute-start(bf16[128,2048]{1,0:T(8,128)(2,1)} %pad_maximum_fusion.7), channel_id=1, source_target_pairs={{0,2},{4,6}} | collective-permute-start | bytes 1572872 | tf_op jit(solution)/shard_map/ppermute | solution.py:104
  694.4 35.5 %collective-permute-start.55 = (bf16[128,2048]{1,0:T(8,128)(2,1)}, bf16[128,2048]{1,0:T(8,128)(2,1)S(1)}, u32[]{:S(2)}, u32[]{:S(2)}) collective-permute-start(bf16[128,2048]{1,0:T(8,128)(2,1)} %pad_maximum_fusion.6), channel_id=1, source_target_pairs={{0,1},{4,5}} | collective-permute-start | bytes 1572872 | tf_op jit(solution)/shard_map/ppermute | solution.py:104
  695.8 34.1 %collective-permute-start.57 = (bf16[128,2048]{1,0:T(8,128)(2,1)}, bf16[128,2048]{1,0:T(8,128)(2,1)S(1)}, u32[]{:S(2)}, u32[]{:S(2)}) collective-permute-start(bf16[128,2048]{1,0:T(8,128)(2,1)} %collective-permute-done.56), channel_id=1, source_target_pairs={{2,3},{6,7}} | collective-permute-start | bytes 1572872 | tf_op jit(solution)/shard_map/ppermute | solution.py:104
  711.9 19.5 %collective-permute-start.60 = (bf16[128,2048]{1,0:T(8,128)(2,1)}, bf16[128,2048]{1,0:T(8,128)(2,1)S(1)}, u32[]{:S(2)}, u32[]{:S(2)}) collective-permute-start(bf16[128,2048]{1,0:T(8,128)(2,1)} %pad_maximum_fusion.7), channel_id=1, source_target_pairs={{0,1},{4,5}} | collective-permute-start | bytes 1572872 | tf_op jit(solution)/shard_map/ppermute | solution.py:104
  713.2 18.1 %collective-permute-start.62 = (bf16[128,2048]{1,0:T(8,128)(2,1)}, bf16[128,2048]{1,0:T(8,128)(2,1)S(1)}, u32[]{:S(2)}, u32[]{:S(2)}) collective-permute-start(bf16[128,2048]{1,0:T(8,128)(2,1)} %collective-permute-done.61), channel_id=1, source_target_pairs={{2,3},{6,7}} | collective-permute-start | bytes 1572872 | tf_op jit(solution)/shard_map/ppermute | solution.py:104
  (81 other events, 774.2 us)

commit v3 on v2

--- a/solution.py
+++ b/solution.py
@@ -1,3 +1,5 @@
+import functools
+
 import jax
 import jax.numpy as jnp
 from jax import lax
@@ -7,7 +9,8 @@
 
 NORM_EPS = 1e-6
 AXES = ('tp', 'pp')
-NUM_CHUNKS = 2
+NUM_CHUNKS = 1
+HIDDEN_BLOCK = 512
 ROW_GROUP = 8
 TABLE_BLOCK = 528
 
@@ -93,6 +96,119 @@
     )(group, used, pick, rows, table)
 
 
+def forward_kernel(x_ref, w_one_ref, w_two_ref, part_ref, *saved):
+    hidden = jnp.dot(x_ref[...], w_one_ref[...], preferred_element_type=jnp.float32)
+    gate_act = jax.nn.gelu(hidden).astype(jnp.bfloat16)
+    update = jnp.dot(gate_act, w_two_ref[...], preferred_element_type=jnp.float32)
+
+    @pl.when(pl.program_id(0) == 0)
+    def _():
+        part_ref[...] = update
+
+    @pl.when(pl.program_id(0) > 0)
+    def _():
+        part_ref[...] += update
+
+    if saved:
+        saved[0][...] = hidden
+        saved[1][...] = gate_act
+
+
+def forward_stage(x_act, w_one, w_two, keep):
+    rows, model_dim = x_act.shape
+    hidden_cols = w_one.shape[1]
+    columns = pl.BlockSpec((rows, HIDDEN_BLOCK), lambda j: (0, j))
+    whole = pl.BlockSpec((rows, model_dim), lambda j: (0, 0))
+    shapes = [jax.ShapeDtypeStruct((rows, model_dim), jnp.float32)]
+    specs = [whole]
+    if keep:
+        shapes += [jax.ShapeDtypeStruct((rows, hidden_cols), jnp.float32), jax.ShapeDtypeStruct((rows, hidden_cols), jnp.bfloat16)]
+        specs += [columns, columns]
+    return pl.pallas_call(
+        forward_kernel,
+        out_shape=shapes,
+        grid=(hidden_cols // HIDDEN_BLOCK,),
+        in_specs=[whole, pl.BlockSpec((model_dim, HIDDEN_BLOCK), lambda j: (0, j)), pl.BlockSpec((HIDDEN_BLOCK, model_dim), lambda j: (j, 0))],
+        out_specs=specs,
+        compiler_params=pltpu.CompilerParams(dimension_semantics=('arbitrary',), vmem_limit_bytes=40 << 20),
+        cost_estimate=pl.CostEstimate(flops=4 * rows * model_dim * hidden_cols, bytes_accessed=4 * model_dim * hidden_cols, transcendentals=rows * hidden_cols),
+        name='forward_stage',
+    )(x_act, w_one, w_two)
+
+
+def backward_kernel(dy_ref, hidden_ref, w_one_ref, w_two_ref, part_ref, dh_ref):
+    grad_gate = lax.dot_general(dy_ref[...], w_two_ref[...], (((1,), (1,)), ((), ())), preferred_element_type=jnp.float32)
+    grad_hidden = jax.vjp(jax.nn.gelu, hidden_ref[...])[1](grad_gate)[0].astype(jnp.bfloat16)
+    dh_ref[...] = grad_hidden
+    update = lax.dot_general(grad_hidden, w_one_ref[...], (((1,), (1,)), ((), ())), preferred_element_type=jnp.float32)
+
+    @pl.when(pl.program_id(0) == 0)
+    def _():
+        part_ref[...] = update
+
+    @pl.when(pl.program_id(0) > 0)
+    def _():
+        part_ref[...] += update
+
+
+def backward_stage(grad_y, hidden, w_one, w_two):
+    rows, model_dim = grad_y.shape
+    hidden_cols = w_one.shape[1]
+    columns = pl.BlockSpec((rows, HIDDEN_BLOCK), lambda j: (0, j))
+    whole = pl.BlockSpec((rows, model_dim), lambda j: (0, 0))
+    return pl.pallas_call(
+        backward_kernel,
+        out_shape=[jax.ShapeDtypeStruct((rows, model_dim), jnp.float32), jax.ShapeDtypeStruct((rows, hidden_cols), jnp.bfloat16)],
+        grid=(hidden_cols // HIDDEN_BLOCK,),
+        in_specs=[whole, columns, pl.BlockSpec((model_dim, HIDDEN_BLOCK), lambda j: (0, j)), pl.BlockSpec((HIDDEN_BLOCK, model_dim), lambda j: (j, 0))],
+        out_specs=[whole, columns],
+        compiler_params=pltpu.CompilerParams(dimension_semantics=('arbitrary',), vmem_limit_bytes=40 << 20),
+        cost_estimate=pl.CostEstimate(flops=4 * rows * model_dim * hidden_cols, bytes_accessed=4 * model_dim * hidden_cols, transcendentals=rows * hidden_cols),
+        name='backward_stage',
+    )(grad_y, hidden, w_one, w_two)
+
+
+def logit_kernel(vocab_rows, emb_ref, normed_ref, label_ref, logit_ref, stat_ref, top_ref, sum_ref, hit_ref):
+    step = pl.program_id(0)
+
+    @pl.when(step == 0)
+    def _():
+        top_ref[...] = jnp.full(top_ref.shape, -jnp.inf, jnp.float32)
+        sum_ref[...] = jnp.zeros(sum_ref.shape, jnp.float32)
+        hit_ref[...] = jnp.zeros(hit_ref.shape, jnp.float32)
+
+    logits = jnp.dot(emb_ref[...], normed_ref[...], preferred_element_type=jnp.float32)
+    logit_ref[...] = logits
+    row_ids = step * TABLE_BLOCK + lax.broadcasted_iota(jnp.int32, logits.shape, 0)
+    inside = row_ids < vocab_rows
+    logits = jnp.where(inside, logits, -jnp.inf)
+    new_top = jnp.maximum(top_ref[...], jnp.max(logits, axis=0, keepdims=True))
+    sum_ref[...] = sum_ref[...] * jnp.exp(top_ref[...] - new_top) + jnp.sum(jnp.exp(logits - new_top), axis=0, keepdims=True)
+    hit_ref[...] += jnp.sum(jnp.where(inside & (row_ids == label_ref[...]), logits, 0.0), axis=0, keepdims=True)
+    top_ref[...] = new_top
+
+    @pl.when(step == pl.num_programs(0) - 1)
+    def _():
+        stat_ref[0:1, :] = top_ref[...] + jnp.log(sum_ref[...])
+        stat_ref[1:2, :] = hit_ref[...]
+
+
+def local_logits(emb_table, normed_b, lab_local):
+    vocab_rows, model_dim = emb_table.shape
+    num_tok = normed_b.shape[0]
+    return pl.pallas_call(
+        functools.partial(logit_kernel, vocab_rows),
+        out_shape=[jax.ShapeDtypeStruct((vocab_rows, num_tok), jnp.float32), jax.ShapeDtypeStruct((2, num_tok), jnp.float32)],
+        grid=(pl.cdiv(vocab_rows, TABLE_BLOCK),),
+        in_specs=[pl.BlockSpec((TABLE_BLOCK, model_dim), lambda i: (i, 0)), pl.BlockSpec((model_dim, num_tok), lambda i: (0, 0)), pl.BlockSpec((1, num_tok), lambda i: (0, 0))],
+        out_specs=[pl.BlockSpec((TABLE_BLOCK, num_tok), lambda i: (i, 0)), pl.BlockSpec((2, num_tok), lambda i: (0, 0))],
+        scratch_shapes=[pltpu.VMEM((1, num_tok), jnp.float32)] * 3,
+        compiler_params=pltpu.CompilerParams(dimension_semantics=('arbitrary',), vmem_limit_bytes=40 << 20),
+        cost_estimate=pl.CostEstimate(flops=2 * vocab_rows * model_dim * num_tok, bytes_accessed=2 * vocab_rows * (model_dim + 2 * num_tok), transcendentals=vocab_rows * num_tok),
+        name='local_logits',
+    )(emb_table, normed_b.T, lab_local.reshape(1, num_tok))
+
+
 def solution(mesh):
     pp_size = mesh.shape['pp']
     last = pp_size - 1
@@ -136,10 +252,12 @@
             return mine(partial) + send(theirs(partial), stage, stage, True)
 
         def spread(value_half, source, far, near, rest):
-            pair = join(value_half, send(value_half, source, source, True))
-            middle = send(pair, source, far, False)
-            others = send(pair, source, near, False) + middle + send(middle, far, rest, False)
-            return jnp.where(stage_idx == source, pair, others)
+            swapped = send(value_half, source, source, True)
+            middle = send(value_half, source, far, False)
+            own = send(value_half, source, near, False) + middle + send(middle, far, rest, False)
+            pairs = [pair for stage in range(pp_size) if stage != source for pair in link(stage, stage, True)]
+            other = lax.ppermute(own, AXES, pairs)
+            return join(jnp.where(stage_idx == source, value_half, own), jnp.where(stage_idx == source, swapped, other))
 
         owned = (tok_local >= 0) & (tok_local < vocab_rows)
         looked_up = jnp.take(emb_table, jnp.clip(tok_local, 0, vocab_rows - 1), axis=0)
@@ -149,9 +267,10 @@
 
         for stage in range(pp_size):
             for c in chunks:
-                hidden[c] = jnp.dot(x_act[c], w_one, preferred_element_type=jnp.float32)
-                gate_act[c] = jax.nn.gelu(hidden[c]).astype(jnp.bfloat16)
-                branch = reduce_half(jnp.dot(gate_act[c], w_two, preferred_element_type=jnp.float32), stage)
+                partial, *saved = forward_stage(x_act[c], w_one, w_two, stage == last)
+                if stage == last:
+                    hidden[c], gate_act[c] = saved
+                branch = reduce_half(partial, stage)
                 y_half[c] = (mine(x_act[c]).astype(jnp.float32) + branch).astype(jnp.bfloat16)
                 if stage < last:
                     arrived = join(send(y_half[c], stage, stage + 1, False), send(y_half[c], stage, stage + 1, True))
@@ -163,12 +282,8 @@
         inv_rms = lax.rsqrt(jnp.mean(x_wide * x_wide, axis=-1, keepdims=True) + NORM_EPS)
         normed = x_wide * inv_rms
         normed_b = normed.astype(jnp.bfloat16)
-        logits = contract(emb_table, normed_b, 1, 1)
+        logits, stats = local_logits(emb_table, normed_b, lab_local)
         target_hit = row_ids[:, None] == lab_local[None, :]
-        local_max = jnp.max(logits, axis=0)
-        local_sum = jnp.sum(jnp.exp(logits - local_max[None, :]), axis=0)
-        local_target = jnp.sum(jnp.where(target_hit, logits, 0.0), axis=0)
-        stats = jnp.stack([jnp.log(local_sum) + local_max, local_target])
         other = lax.ppermute(stats, 'tp', [(0, 1), (1, 0)])
         log_norm = jnp.logaddexp(stats[0], other[0])
         mean_loss = jnp.sum(log_norm - (stats[1] + other[1])) / num_tok
@@ -192,8 +307,8 @@
 
                 def run_stage(operands):
                     dy, wide, kept, held = operands
-                    dh = jax.vjp(jax.nn.gelu, wide)[1](contract(dy, w_two, 1, 1))[0].astype(jnp.bfloat16)
-                    return contract(dh, w_one, 1, 1), dh, held
+                    part, dh = backward_stage(dy, wide, w_one, w_two)
+                    return part, dh, held
 
                 def fill_table(operands):
                     dy, wide, kept, held = operands

time: 758 us -> 664 us (0.88)
  matrix products: 301 us -> 70.8 us
  Pallas kernels: 95.6 us -> 250 us
  waiting for transfers between devices: 160 us -> 215 us
  starting transfers between devices: 85.8 us -> 49.5 us
  other arithmetic: 67.6 us -> 47.8 us
  local copies, waits for them, and re-layouts: 33.7 us -> 17 us
    pallas_call x0 -> x6, Pallas kernels: none -> 161 us  [the longest x4 71.9 us: forward_stage(): pl.pallas_call(forward_kernel, out_shape=shapes, grid=(hidden_cols // HID...]
    dot_general x10 -> x0, matrix products: 127 us -> none  [the longest x8 113 us: device_fn(): jnp.dot(gate_act[c], w_two, preferred_element_type=jnp.float32)]
    dot_general x8 -> x3, matrix products: 173 us -> 70.8 us  [contract(): lax.dot_general(lhs, rhs, (((lhs_dim,), (rhs_dim,)), ((), ())), preferred...]
    ppermute x62 -> x31, waiting for transfers between devices: 156 us -> 199 us  [send(): return lax.ppermute(value, AXES, link(src_stage, dst_stage, cross))]
    ppermute x62 -> x31, starting transfers between devices: 83.6 us -> 46.4 us  [send(): return lax.ppermute(value, AXES, link(src_stage, dst_stage, cross))]
    ppermute x0 -> x2, waiting for transfers between devices: none -> 13.6 us  [spread(): other = lax.ppermute(own, AXES, pairs)]
    reduce_sum x1 -> x0, other arithmetic: 13.2 us -> none  [device_fn(): local_sum = jnp.sum(jnp.exp(logits - local_max[None, :]), axis=0)]
    dynamic_slice x18 -> x9, local copies, waits for them, and re-layouts: 13.3 us -> 3.15 us  [theirs(): return lax.dynamic_slice_in_dim(value, (1 - tp_idx) * half, half, 0)]
  transfers between devices with their start and end apart: 63 -> 34, of which waited for: 10 -> 11; matrix products, arithmetic and copies ran while one was open for 33% -> 5% of each run, Pallas kernels for 11% -> 0%
where the time goes in v3:
time: 664 us; the launch traced here: 655 us
  Pallas kernels  250 us (38%)
  waiting for transfers between devices  215 us (32%)
  matrix products  70.8 us (11%)
  starting transfers between devices  49.5 us (7%)
  other arithmetic  47.8 us (7%)
  local copies, waits for them, and re-layouts  17 us (3%)
    ppermute x31, waiting for transfers between devices, send(): return lax.ppermute(value, AXES, link(src_stage, dst_stage, cross))  199 us
    pallas_call x3, Pallas kernels, head_rows(): pl.pallas_call(head_kernel, out_shape=jax.ShapeDtypeStruct(table.shape, t...  73.5 us
    pallas_call x4, Pallas kernels, forward_stage(): pl.pallas_call(forward_kernel, out_shape=shapes, grid=(hidden_cols // HID...  71.9 us
    dot_general x3, matrix products, contract(): lax.dot_general(lhs, rhs, (((lhs_dim,), (rhs_dim,)), ((), ())), preferred...  70.8 us
    pallas_call x1, Pallas kernels, local_logits(): pl.pallas_call(functools.partial(logit_kernel, vocab_rows), out_shape=[ja...  68.5 us
    ppermute x31, starting transfers between devices, send(): return lax.ppermute(value, AXES, link(src_stage, dst_stage, cross))  46.4 us
    pallas_call x1, Pallas kernels, backward_stage(): pl.pallas_call(backward_kernel, out_shape=[jax.ShapeDtypeStruct((rows, mo...  20.9 us
    convert_element_type x1, other arithmetic, device_fn(): (jnp.exp(logits - log_norm[None, :]) - target_hit.astype(jnp.float32)).as...  15.5 us
  transfers between devices with their start and end apart: 34, of which 11 were waited for; matrix products, arithmetic and copies ran while one was open for 5% of the time, Pallas kernels for 0%

profile of v3, /device:TPU:0, one launch (start us, length us, event | category | flops | bytes accessed | tf_op | source)
XLA Modules:
  0.0 654.6 jit_solution(17375667320937312058)
XLA Ops:
  3.4 7.6 %gather_fusion = bf16[256,2048]{1,0:T(8,128)(2,1)S(1)} fusion(bf16[25136,2048]{1,0:T(8,128)(2,1)} %emb_ref.1, s32[1024]{0:T(1024)S(1)} %pad_clamp_fusion), kind=kCustom, calls=%fused_computation | custom fusion | bytes 2098176 | tf_op jit(solution)/shard_map/jit(_take)/gather | solution.py:263
  11.2 5.6 collective-permute-start
  16.8 12.8 %collective-permute-done = bf16[256,2048]{1,0:T(8,128)(2,1)S(1)} collective-permute-done((bf16[256,2048]{1,0:T(8,128)(2,1)S(1)}, bf16[256,2048]{1,0:T(8,128)(2,1)S(1)}, u32[]{:S(2)}, u32[]{:S(2)}) %collective-permute-start) | collective-permute-done | bytes 1048608 | tf_op jit(solution)/shard_map/ppermute | solution.py:220
  29.8 17.5 %forward_stage.4 = f32[256,2048]{1,0:T(8,128)S(1)} custom-call(bf16[256,2048]{1,0:T(8,128)(2,1)S(1)} %fusion.14.x_ref, bf16[2048,4096]{1,0:T(8,128)(2,1)} %bitcast.20, bf16[4096,2048]{1,0:T(8,128)(2,1)} %bitcast.28), custom_call_target="tpu_custom_call" | custom-call | flops 8589934592 | bytes 33554432 | tf_op jit(solution)/shard_map/forward_stage/pallas_call | solution.py:127
  48.3 3.9 collective-permute-start.1
  52.2 12.8 %collective-permute-done.1 = f32[128,2048]{1,0:T(8,128)} collective-permute-done((f32[128,2048]{1,0:T(8,128)}, f32[128,2048]{1,0:T(8,128)}, u32[]{:S(2)}, u32[]{:S(2)}) %collective-permute-start.1) | collective-permute-done | bytes 1048608 | tf_op jit(solution)/shard_map/ppermute | solution.py:220
  70.0 6.5 collective-permute-done.3
  76.9 17.5 %forward_stage.5 = f32[256,2048]{1,0:T(8,128)S(1)} custom-call(bf16[256,2048]{1,0:T(8,128)(2,1)S(1)} %maximum_select_fusion.x_ref, bf16[2048,4096]{1,0:T(8,128)(2,1)} %bitcast.21, bf16[4096,2048]{1,0:T(8,128)(2,1)} %bitcast.29), custom_call_target="tpu_custom_call" | custom-call | flops 8589934592 | bytes 33554432 | tf_op jit(solution)/shard_map/forward_stage/pallas_call | solution.py:127
  97.3 17.5 %forward_stage.6 = f32[256,2048]{1,0:T(8,128)S(1)} custom-call(bf16[256,2048]{1,0:T(8,128)(2,1)S(1)} %maximum_select_fusion.1.x_ref, bf16[2048,4096]{1,0:T(8,128)(2,1)} %bitcast.22, bf16[4096,2048]{1,0:T(8,128)(2,1)} %bitcast.30), custom_call_target="tpu_custom_call" | custom-call | flops 8589934592 | bytes 33554432 | tf_op jit(solution)/shard_map/forward_stage/pallas_call | solution.py:127
  117.9 19.5 %forward_stage.7 = (f32[256,2048]{1,0:T(8,128)S(1)}, f32[256,4096]{1,0:T(8,128)}, bf16[256,4096]{1,0:T(8,128)(2,1)S(1)}) custom-call(bf16[256,2048]{1,0:T(8,128)(2,1)S(1)} %maximum_select_fusion.2.x_ref, bf16[2048,4096]{1,0:T(8,128)(2,1)} %bitcast.23, bf16[4096,2048]{1,0:T(8,128)(2,1)} %bitcast.31), custom_call_target="tpu_custom_call" | custom-call | flops 8589934592 | bytes 33554432 | tf_op jit(solution)/shard_map/forward_stage/pallas_call | solution.py:127
  142.7 77.2 %collective-permute-done.13 = bf16[128,2048]{1,0:T(8,128)(2,1)S(1)} collective-permute-done((bf16[128,2048]{1,0:T(8,128)(2,1)S(1)}, bf16[128,2048]{1,0:T(8,128)(2,1)S(1)}, u32[]{:S(2)}, u32[]{:S(2)}) %collective-permute-start.13) | collective-permute-done | bytes 524320 | tf_op jit(solution)/shard_map/ppermute | solution.py:220
  222.3 13.6 %collective-permute-done.15 = bf16[128,2048]{1,0:T(8,128)(2,1)} collective-permute-done((bf16[128,2048]{1,0:T(8,128)(2,1)S(1)}, bf16[128,2048]{1,0:T(8,128)(2,1)}, u32[]{:S(2)}, u32[]{:S(2)}) %collective-permute-start.15) | collective-permute-done | bytes 524320 | tf_op jit(solution)/shard_map/ppermute | solution.py:259
  240.8 68.5 %local_logits.1 = (f32[25136,256]{1,0:T(8,128)}, f32[2,256]{1,0:T(2,128)S(1)}) custom-call(bf16[25136,2048]{1,0:T(8,128)(2,1)} %emb_ref.1, bf16[2048,256]{1,0:T(8,128)(2,1)S(1)} %copy.16.normed_ref, s32[1,256]{1,0:T(1,128)S(1)} %sub.130.label_ref), custom_call_target="tpu_custom_call" | custom-call | flops 26357006336 | bytes 128696320 | tf_op jit(solution)/shard_map/local_logits/pallas_call | solution.py:199
  309.7 3.2 collective-permute-done.16
  313.5 15.5 %subtract_convert_fusion = bf16[25136,256]{1,0:T(8,128)(2,1)} fusion(f32[25136,256]{1,0:T(8,128)} %get-tuple-element.228, s32[256]{0:T(256)S(1)} %sub.137, f32[256]{0:T(256)S(1)} %bitcast.37), kind=kLoop, calls=%fused_computation.1 | loop fusion | flops 32174080 | bytes 38610944 | tf_op jit(solution)/shard_map/convert_element_type | solution.py:290
  329.0 41.2 %fusion.7 = f32[256,2048]{1,0:T(8,128)} fusion(bf16[25136,256]{1,0:T(8,128)(2,1)} %subtract_convert_fusion, bf16[25136,2048]{1,0:T(8,128)(2,1)} %emb_ref.1), kind=kOutput, calls=%fused_computation.92 | convolution fusion | flops 26357006336 | bytes 117923840 | tf_op jit(solution)/shard_map/dot_general | solution.py:19
  379.5 26.7 %conditional.4 = (f32[256,2048]{1,0:T(8,128)S(1)}, bf16[256,4096]{1,0:T(8,128)(2,1)}, f32[25136,2048]{1,0:T(8,128)}) conditional(s32[]{:T(128)} %convert_element_type.97, (s32[]{:T(128)}, bf16[25136,256]{1,0:T(8,128)(2,1)}, bf16[256,2048]{1,0:T(8,128)(2,1)S(1)}, f32[25136,2048]{1,0:T(8,128)}) %tuple.89, (bf16[256,2048]{1,0:T(8,128)(2,1)}, ...), branch_computations={%region_3.4_spmd, %region_4.5_spmd} | conditional | flops 8858370048 | bytes 73400392 | solution.py:318
  379.5 24.7 %head_rows.8 = f32[25136,2048]{1,0:T(8,128)} custom-call(s32[1]{0:T(128)} %bitcast.base_ref, bf16[25136,256]{1,0:T(8,128)(2,1)} %get-tuple-element.159.grad_ref, bf16[256,2048]{1,0:T(8,128)(2,1)S(1)} %get-tuple-element.160.normed_ref, f32[25136,2048]{1,0:T(8,128)} %get-tuple-element.161.table_in), custom_call_target="tpu_custom_call", output_to_operand_aliasing={{}: (3, {})} | custom-call | flops 8858370048 | bytes 69206016 | tf_op jit(solution)/shard_map/cond/branch_0_fun/head_rows/pallas_call | solution.py:33
  414.4 24.9 %conditional.5 = (f32[256,2048]{1,0:T(8,128)S(1)}, bf16[256,4096]{1,0:T(8,128)(2,1)}, f32[25136,2048]{1,0:T(8,128)}) conditional(s32[]{:T(128)} %convert_element_type.96, (s32[]{:T(128)}, bf16[25136,256]{1,0:T(8,128)(2,1)}, bf16[256,2048]{1,0:T(8,128)(2,1)S(1)}, f32[25136,2048]{1,0:T(8,128)}, bf16[256,4096]{1,0:T(8,128)(2,1)}) %tuple.90, ...), branch_computations={%region_5.6_spmd, %region_6.7_spmd} | conditional | flops 8858370048 | bytes 71303240 | solution.py:318
  414.4 24.7 %head_rows.9 = f32[25136,2048]{1,0:T(8,128)} custom-call(s32[1]{0:T(128)} %bitcast.1.base_ref, bf16[25136,256]{1,0:T(8,128)(2,1)} %get-tuple-element.171.grad_ref, bf16[256,2048]{1,0:T(8,128)(2,1)S(1)} %get-tuple-element.172.normed_ref, f32[25136,2048]{1,0:T(8,128)} %get-tuple-element.173.table_in), custom_call_target="tpu_custom_call", output_to_operand_aliasing={{}: (3, {})} | custom-call | flops 8858370048 | bytes 69206016 | tf_op jit(solution)/shard_map/cond/branch_0_fun/head_rows/pallas_call | solution.py:33
  447.4 24.4 %conditional.6 = (f32[256,2048]{1,0:T(8,128)S(1)}, bf16[256,4096]{1,0:T(8,128)(2,1)}, f32[25136,2048]{1,0:T(8,128)}) conditional(s32[]{:T(128)} %convert_element_type.95, (s32[]{:T(128)}, bf16[25136,256]{1,0:T(8,128)(2,1)}, bf16[256,2048]{1,0:T(8,128)(2,1)S(1)}, f32[25136,2048]{1,0:T(8,128)}, bf16[256,4096]{1,0:T(8,128)(2,1)}) %tuple.91, ...), branch_computations={%region_7.8_spmd, %region_8.9_spmd} | conditional | flops 8858370048 | bytes 71303240 | solution.py:318
  447.4 24.1 %head_rows.10 = f32[25136,2048]{1,0:T(8,128)} custom-call(s32[1]{0:T(128)} %bitcast.2.base_ref, bf16[25136,256]{1,0:T(8,128)(2,1)} %get-tuple-element.183.grad_ref, bf16[256,2048]{1,0:T(8,128)(2,1)S(1)} %get-tuple-element.184.normed_ref, f32[25136,2048]{1,0:T(8,128)} %get-tuple-element.185.table_in), custom_call_target="tpu_custom_call", output_to_operand_aliasing={{}: (3, {})} | custom-call | flops 8858370048 | bytes 69206016 | tf_op jit(solution)/shard_map/cond/branch_0_fun/head_rows/pallas_call | solution.py:33
  476.6 66.8 %collective-permute-done.26 = bf16[128,2048]{1,0:T(8,128)(2,1)} collective-permute-done((bf16[128,2048]{1,0:T(8,128)(2,1)}, bf16[128,2048]{1,0:T(8,128)(2,1)}, u32[]{:S(2)}, u32[]{:S(2)}) %collective-permute-start.26) | collective-permute-done | bytes 524320 | tf_op jit(solution)/shard_map/ppermute | solution.py:220
  543.4 7.5 %collective-permute-done.27 = bf16[128,2048]{1,0:T(8,128)(2,1)} collective-permute-done((bf16[128,2048]{1,0:T(8,128)(2,1)}, bf16[128,2048]{1,0:T(8,128)(2,1)}, u32[]{:S(2)}, u32[]{:S(2)}) %collective-permute-start.27) | collective-permute-done | bytes 524320 | tf_op jit(solution)/shard_map/ppermute | solution.py:220
  553.7 21.1 %conditional.7 = (f32[256,2048]{1,0:T(8,128)S(1)}, bf16[256,4096]{1,0:T(8,128)(2,1)}, f32[25136,2048]{1,0:T(8,128)}) conditional(s32[]{:T(128)} %convert_element_type.92, (s32[]{:T(128)}, bf16[25136,256]{1,0:T(8,128)(2,1)}, bf16[256,2048]{1,0:T(8,128)(2,1)S(1)}, f32[25136,2048]{1,0:T(8,128)}, bf16[256,4096]{1,0:T(8,128)(2,1)}) %tuple.92, ...), branch_computations={%region_9.10_spmd, %region_10.11_spmd} | conditional | flops 8858370048 | bytes 71303240 | solution.py:318
  553.9 20.9 %backward_stage.7 = (f32[256,2048]{1,0:T(8,128)S(1)}, bf16[256,4096]{1,0:T(8,128)(2,1)}) custom-call(bf16[256,2048]{1,0:T(8,128)(2,1)} %get-tuple-element.198.dy_ref, f32[256,4096]{1,0:T(8,128)} %get-tuple-element.199.hidden_ref, bf16[2048,4096]{1,0:T(8,128)(2,1)} %get-tuple-element.200.w_one_ref, bf16[4096,2048]{1,0:T(8,128)(2,1)} %get-tuple-element.201.w_two_ref), custom_call_target="tpu_custom_call" | custom-call | flops 8589934592 | bytes 33554432 | tf_op jit(solution)/shard_map/cond/branch_1_fun/backward_stage/pallas_call | solution.py:159
  574.9 3.8 collective-permute-start.28
  578.8 12.9 %collective-permute-done.28 = f32[128,2048]{1,0:T(8,128)S(1)} collective-permute-done((f32[128,2048]{1,0:T(8,128)S(1)}, f32[128,2048]{1,0:T(8,128)S(1)}, u32[]{:S(2)}, u32[]{:S(2)}) %collective-permute-start.28) | collective-permute-done | bytes 1048608 | tf_op jit(solution)/shard_map/ppermute | solution.py:220
  601.4 15.5 %convolution_bitcast_fusion = f32[1,4096,2048]{2,1,0:T(8,128)} fusion(bf16[256,4096]{1,0:T(8,128)(2,1)S(1)} %get-tuple-element.240, bf16[256,2048]{1,0:T(8,128)(2,1)} %maximum_select_fusion.5), kind=kOutput, calls=%fused_computation.3 | convolution fusion | flops 4294967296 | bytes 36700160 | tf_op jit(solution)/shard_map/dot_general | solution.py:19
  616.9 3.8 collective-permute-start.32
  622.5 14.1 %convolution_bitcast_fusion.1 = f32[1,2048,4096]{2,1,0:T(8,128)} fusion(bf16[256,2048]{1,0:T(8,128)(2,1)S(1)} %copy-done.1, bf16[256,4096]{1,0:T(8,128)(2,1)S(1)} %copy-done.10), kind=kOutput, calls=%fused_computation.4 | convolution fusion | flops 4294967296 | bytes 36700160 | tf_op jit(solution)/shard_map/dot_general | solution.py:19
  637.9 15.1 %add_rows.1 = f32[25136,2048]{1,0:T(8,128)} custom-call(s32[256]{0:T(256)S(1)} %broadcast_maximum_fusion.group_ref, s32[256]{0:T(256)S(1)} %get-tuple-element.244.used_ref, bf16[2048,256]{1,0:T(8,128)(2,1)S(1)} %and_convert_fusion.pick_ref, bf16[256,2048]{1,0:T(8,128)(2,1)S(1)} %pad_maximum_fusion.2.rows_ref, ...), custom_call_target="tpu_custom_call", output_to_operand_aliasing={{}: (4, {})} | custom-call | tf_op jit(solution)/shard_map/add_rows/pallas_call | solution.py:87
  (172 shorter events, 76.5 us)
Async XLA Ops:
  11.2 18.3 %collective-permute-start = (bf16[256,2048]{1,0:T(8,128)(2,1)S(1)}, bf16[256,2048]{1,0:T(8,128)(2,1)S(1)}, u32[]{:S(2)}, u32[]{:S(2)}) collective-permute-start(bf16[256,2048]{1,0:T(8,128)(2,1)S(1)} %select_select_fusion), channel_id=1, source_target_pairs={{0,4},{4,0}} | collective-permute-start | bytes 3145736 | tf_op jit(solution)/shard_map/ppermute | solution.py:220
  48.3 16.7 %collective-permute-start.1 = (f32[128,2048]{1,0:T(8,128)}, f32[128,2048]{1,0:T(8,128)}, u32[]{:S(2)}, u32[]{:S(2)}) collective-permute-start(f32[128,2048]{1,0:T(8,128)} %constant_dynamic-slice_fusion.7), channel_id=1, source_target_pairs={{0,4},{4,0}} | collective-permute-start | bytes 3145736 | tf_op jit(solution)/shard_map/ppermute | solution.py:220
  67.2 2.8 collective-permute-start.2
  68.5 8.0 %collective-permute-start.3 = (bf16[128,2048]{1,0:T(8,128)(2,1)}, bf16[128,2048]{1,0:T(8,128)(2,1)S(1)}, u32[]{:S(2)}, u32[]{:S(2)}) collective-permute-start(bf16[128,2048]{1,0:T(8,128)(2,1)} %add_convert_fusion.7), channel_id=1, source_target_pairs={{0,5},{4,1}} | collective-permute-start | bytes 1572872 | tf_op jit(solution)/shard_map/ppermute | solution.py:220
  94.5 0.7 collective-permute-start.4
  95.4 1.4 collective-permute-start.5
  114.9 0.7 collective-permute-start.7
  115.8 1.6 collective-permute-start.8
  116.5 0.9 collective-permute-start.9
  138.5 1.4 collective-permute-start.12
  139.2 3.5 collective-permute-start.11
  139.9 80.0 %collective-permute-start.13 = (bf16[128,2048]{1,0:T(8,128)(2,1)S(1)}, bf16[128,2048]{1,0:T(8,128)(2,1)S(1)}, u32[]{:S(2)}, u32[]{:S(2)}) collective-permute-start(bf16[128,2048]{1,0:T(8,128)(2,1)S(1)} %collective-permute-done.12), channel_id=1, source_target_pairs={{1,0},{5,4}} | collective-permute-start | bytes 1572872 | tf_op jit(solution)/shard_map/ppermute | solution.py:220
  141.2 81.1 %collective-permute-start.14 = (bf16[128,2048]{1,0:T(8,128)(2,1)S(1)}, bf16[128,2048]{1,0:T(8,128)(2,1)}, u32[]{:S(2)}, u32[]{:S(2)}) collective-permute-start(bf16[128,2048]{1,0:T(8,128)(2,1)S(1)} %add_convert_fusion.4), channel_id=1, source_target_pairs={{3,7},{7,3}} | collective-permute-start | bytes 1572872 | tf_op jit(solution)/shard_map/ppermute | solution.py:220
  220.0 15.9 %collective-permute-start.15 = (bf16[128,2048]{1,0:T(8,128)(2,1)S(1)}, bf16[128,2048]{1,0:T(8,128)(2,1)}, u32[]{:S(2)}, u32[]{:S(2)}) collective-permute-start(bf16[128,2048]{1,0:T(8,128)(2,1)S(1)} %add_add_fusion.1), channel_id=1, source_target_pairs={{0,4},{4,0},{1,5},{5,1},{2,6},{6,2}} | collective-permute-start | bytes 1572872 | tf_op jit(solution)/shard_map/ppermute | solution.py:259
  309.3 3.6 collective-permute-start.16
  371.7 0.9 collective-permute-start.17
  375.3 1.5 collective-permute-start.18
  406.3 0.9 collective-permute-start.19
  408.6 2.9 collective-permute-start.20
  410.1 1.5 collective-permute-start.21
  439.4 0.9 collective-permute-start.22
  441.6 2.9 collective-permute-start.23
  443.1 1.5 collective-permute-start.24
  471.9 0.9 collective-permute-start.25
  474.0 69.4 %collective-permute-start.26 = (bf16[128,2048]{1,0:T(8,128)(2,1)}, bf16[128,2048]{1,0:T(8,128)(2,1)}, u32[]{:S(2)}, u32[]{:S(2)}) collective-permute-start(bf16[128,2048]{1,0:T(8,128)(2,1)} %add_convert_fusion.1), channel_id=1, source_target_pairs={{1,0},{5,4}} | collective-permute-start | bytes 1572872 | tf_op jit(solution)/shard_map/ppermute | solution.py:220
  475.3 75.6 %collective-permute-start.27 = (bf16[128,2048]{1,0:T(8,128)(2,1)}, bf16[128,2048]{1,0:T(8,128)(2,1)}, u32[]{:S(2)}, u32[]{:S(2)}) collective-permute-start(bf16[128,2048]{1,0:T(8,128)(2,1)} %add_convert_fusion.1), channel_id=1, source_target_pairs={{1,4},{5,0}} | collective-permute-start | bytes 1572872 | tf_op jit(solution)/shard_map/ppermute | solution.py:220
  574.9 16.8 %collective-permute-start.28 = (f32[128,2048]{1,0:T(8,128)S(1)}, f32[128,2048]{1,0:T(8,128)S(1)}, u32[]{:S(2)}, u32[]{:S(2)}) collective-permute-start(f32[128,2048]{1,0:T(8,128)S(1)} %constant_dynamic-slice_fusion), channel_id=1, source_target_pairs={{0,4},{4,0}} | collective-permute-start | bytes 3145736 | tf_op jit(solution)/shard_map/ppermute | solution.py:220
  592.8 7.9 %collective-permute-start.30 = (bf16[128,2048]{1,0:T(8,128)(2,1)}, bf16[128,2048]{1,0:T(8,128)(2,1)}, u32[]{:S(2)}, u32[]{:S(2)}) collective-permute-start(bf16[128,2048]{1,0:T(8,128)(2,1)} %add_convert_fusion), channel_id=1, source_target_pairs={{0,2},{4,6}} | collective-permute-start | bytes 1572872 | tf_op jit(solution)/shard_map/ppermute | solution.py:220
  597.3 23.3 %collective-permute-start.29 = (bf16[128,2048]{1,0:T(8,128)(2,1)}, bf16[128,2048]{1,0:T(8,128)(2,1)S(1)}, u32[]{:S(2)}, u32[]{:S(2)}) collective-permute-start(bf16[128,2048]{1,0:T(8,128)(2,1)} %add_convert_fusion), channel_id=1, source_target_pairs={{0,1},{4,5}} | collective-permute-start | bytes 1572872 | tf_op jit(solution)/shard_map/ppermute | solution.py:220
  600.7 19.9 %collective-permute-start.31 = (bf16[128,2048]{1,0:T(8,128)(2,1)}, bf16[128,2048]{1,0:T(8,128)(2,1)S(1)}, u32[]{:S(2)}, u32[]{:S(2)}) collective-permute-start(bf16[128,2048]{1,0:T(8,128)(2,1)} %collective-permute-done.30), channel_id=1, source_target_pairs={{2,3},{6,7}} | collective-permute-start | bytes 1572872 | tf_op jit(solution)/shard_map/ppermute | solution.py:220
  616.9 19.7 %collective-permute-start.32 = (bf16[128,2048]{1,0:T(8,128)(2,1)}, bf16[128,2048]{1,0:T(8,128)(2,1)S(1)}, u32[]{:S(2)}, u32[]{:S(2)}) collective-permute-start(bf16[128,2048]{1,0:T(8,128)(2,1)} %add_convert_fusion), channel_id=1, source_target_pairs={{0,4},{4,0}} | collective-permute-start | bytes 1572872 | tf_op jit(solution)/shard_map/ppermute | solution.py:220
  621.8 14.8 %collective-permute-start.33 = (bf16[128,2048]{1,0:T(8,128)(2,1)S(1)}, bf16[128,2048]{1,0:T(8,128)(2,1)S(1)}, u32[]{:S(2)}, u32[]{:S(2)}) collective-permute-start(bf16[128,2048]{1,0:T(8,128)(2,1)S(1)} %add_add_fusion), channel_id=1, source_target_pairs={{1,5},{5,1},{2,6},{6,2},{3,7},{7,3}} | collective-permute-start | bytes 1572872 | tf_op jit(solution)/shard_map/ppermute | solution.py:259
  (26 other events, 319.4 us)

commit v4 on v2

--- a/solution.py
+++ b/solution.py
@@ -7,7 +7,8 @@
 
 NORM_EPS = 1e-6
 AXES = ('tp', 'pp')
-NUM_CHUNKS = 2
+NUM_CHUNKS = 1
+HIDDEN_BLOCK = 512
 ROW_GROUP = 8
 TABLE_BLOCK = 528
 
@@ -93,6 +94,38 @@
     )(group, used, pick, rows, table)
 
 
+def backward_kernel(dy_ref, hidden_ref, w_one_ref, w_two_ref, part_ref, dh_ref):
+    grad_gate = lax.dot_general(dy_ref[...], w_two_ref[...], (((1,), (1,)), ((), ())), preferred_element_type=jnp.float32)
+    grad_hidden = jax.vjp(jax.nn.gelu, hidden_ref[...])[1](grad_gate)[0].astype(jnp.bfloat16)
+    dh_ref[...] = grad_hidden
+    update = lax.dot_general(grad_hidden, w_one_ref[...], (((1,), (1,)), ((), ())), preferred_element_type=jnp.float32)
+
+    @pl.when(pl.program_id(0) == 0)
+    def _():
+        part_ref[...] = update
+
+    @pl.when(pl.program_id(0) > 0)
+    def _():
+        part_ref[...] += update
+
+
+def backward_stage(grad_y, hidden, w_one, w_two):
+    rows, model_dim = grad_y.shape
+    hidden_cols = w_one.shape[1]
+    columns = pl.BlockSpec((rows, HIDDEN_BLOCK), lambda j: (0, j))
+    whole = pl.BlockSpec((rows, model_dim), lambda j: (0, 0))
+    return pl.pallas_call(
+        backward_kernel,
+        out_shape=[jax.ShapeDtypeStruct((rows, model_dim), jnp.float32), jax.ShapeDtypeStruct((rows, hidden_cols), jnp.bfloat16)],
+        grid=(hidden_cols // HIDDEN_BLOCK,),
+        in_specs=[whole, columns, pl.BlockSpec((model_dim, HIDDEN_BLOCK), lambda j: (0, j)), pl.BlockSpec((HIDDEN_BLOCK, model_dim), lambda j: (j, 0))],
+        out_specs=[whole, columns],
+        compiler_params=pltpu.CompilerParams(dimension_semantics=('arbitrary',), vmem_limit_bytes=40 << 20),
+        cost_estimate=pl.CostEstimate(flops=4 * rows * model_dim * hidden_cols, bytes_accessed=4 * model_dim * hidden_cols, transcendentals=rows * hidden_cols),
+        name='backward_stage',
+    )(grad_y, hidden, w_one, w_two)
+
+
 def solution(mesh):
     pp_size = mesh.shape['pp']
     last = pp_size - 1
@@ -136,10 +169,12 @@
             return mine(partial) + send(theirs(partial), stage, stage, True)
 
         def spread(value_half, source, far, near, rest):
-            pair = join(value_half, send(value_half, source, source, True))
-            middle = send(pair, source, far, False)
-            others = send(pair, source, near, False) + middle + send(middle, far, rest, False)
-            return jnp.where(stage_idx == source, pair, others)
+            swapped = send(value_half, source, source, True)
+            middle = send(value_half, source, far, False)
+            own = send(value_half, source, near, False) + middle + send(middle, far, rest, False)
+            pairs = [pair for stage in range(pp_size) if stage != source for pair in link(stage, stage, True)]
+            other = lax.ppermute(own, AXES, pairs)
+            return join(jnp.where(stage_idx == source, value_half, own), jnp.where(stage_idx == source, swapped, other))
 
         owned = (tok_local >= 0) & (tok_local < vocab_rows)
         looked_up = jnp.take(emb_table, jnp.clip(tok_local, 0, vocab_rows - 1), axis=0)
@@ -149,7 +184,7 @@
 
         for stage in range(pp_size):
             for c in chunks:
-                hidden[c] = jnp.dot(x_act[c], w_one, preferred_element_type=jnp.float32)
+                hidden[c] = lax.optimization_barrier(jnp.dot(x_act[c], w_one, preferred_element_type=jnp.float32))
                 gate_act[c] = jax.nn.gelu(hidden[c]).astype(jnp.bfloat16)
                 branch = reduce_half(jnp.dot(gate_act[c], w_two, preferred_element_type=jnp.float32), stage)
                 y_half[c] = (mine(x_act[c]).astype(jnp.float32) + branch).astype(jnp.bfloat16)
@@ -192,8 +227,8 @@
 
                 def run_stage(operands):
                     dy, wide, kept, held = operands
-                    dh = jax.vjp(jax.nn.gelu, wide)[1](contract(dy, w_two, 1, 1))[0].astype(jnp.bfloat16)
-                    return contract(dh, w_one, 1, 1), dh, held
+                    part, dh = backward_stage(dy, wide, w_one, w_two)
+                    return part, dh, held
 
                 def fill_table(operands):
                     dy, wide, kept, held = operands
@@ -201,13 +236,16 @@
                     return jnp.zeros(dy.shape, jnp.float32), kept, head_rows(base, grad_logits, normed_b, held, fill_steps)
 
                 partial, grad_hidden[c], table = lax.cond(stage_idx == stage, run_stage, fill_table, (grad_y[c], hidden[c], grad_hidden[c], table))
-                dx_half[c] = (mine(grad_y[c]).astype(jnp.float32) + reduce_half(partial, stage)).astype(jnp.bfloat16)
+                branch = reduce_half(partial, stage)
+                if stage == 0:
+                    grad_two = contract(gate_act[c], grad_y[c], 0, 0)
+                    branch, grad_two = lax.optimization_barrier((branch, grad_two))
+                dx_half[c] = (mine(grad_y[c]).astype(jnp.float32) + branch).astype(jnp.bfloat16)
                 if stage > 0:
                     arrived = join(send(dx_half[c], stage, stage - 1, False), send(dx_half[c], stage, stage - 1, True))
                     grad_y[c] = jnp.where(stage_idx == stage - 1, arrived, grad_y[c])
 
         dx_rows = jnp.concatenate([spread(dx_half[c], 0, 2, 1, 3) for c in chunks], axis=0)
-        grad_two = contract(jnp.concatenate(gate_act, axis=0), jnp.concatenate(grad_y, axis=0), 0, 0)
         grad_one = contract(jnp.concatenate(x_act, axis=0), jnp.concatenate(grad_hidden, axis=0), 0, 0)
         slot_ids = jnp.arange(num_tok, dtype=jnp.int32)
         group = jnp.where(owned, tok_local // ROW_GROUP, -1)

time: 758 us -> 621 us (0.82)
  matrix products: 301 us -> 177 us
  waiting for transfers between devices: 160 us -> 206 us
  starting transfers between devices: 85.8 us -> 45 us
  other arithmetic: 67.6 us -> 48.4 us
  Pallas kernels: 95.6 us -> 109 us
  local copies, waits for them, and re-layouts: 33.7 us -> 22.4 us
    dot_general x8 -> x4, matrix products: 113 us -> 20 us  [device_fn(): jnp.dot(gate_act[c], w_two, preferred_element_type=jnp.float32)]
    dot_general x8 -> x4, matrix products: 173 us -> 123 us  [contract(): lax.dot_general(lhs, rhs, (((lhs_dim,), (rhs_dim,)), ((), ())), preferred...]
    ppermute x62 -> x31, starting transfers between devices: 83.6 us -> 41.6 us  [send(): return lax.ppermute(value, AXES, link(src_stage, dst_stage, cross))]
    ppermute x62 -> x31, waiting for transfers between devices: 156 us -> 190 us  [send(): return lax.ppermute(value, AXES, link(src_stage, dst_stage, cross))]
    pallas_call x0 -> x1, Pallas kernels: none -> 20.2 us  [backward_stage(): pl.pallas_call(backward_kernel, out_shape=[jax.ShapeDtypeStruct((rows, mo...]
    dot_general x2 -> x4, matrix products: 14.7 us -> 33.9 us  [device_fn(): jnp.dot(x_act[c], w_one, preferred_element_type=jnp.float32)]
    ppermute x0 -> x2, waiting for transfers between devices: none -> 13.4 us  [spread(): other = lax.ppermute(own, AXES, pairs)]
    dynamic_slice x18 -> x9, local copies, waits for them, and re-layouts: 13.3 us -> 0.77 us  [theirs(): return lax.dynamic_slice_in_dim(value, (1 - tp_idx) * half, half, 0)]
  transfers between devices with their start and end apart: 63 -> 34, of which waited for: 10 -> 9; matrix products, arithmetic and copies ran while one was open for 33% -> 6% of each run, Pallas kernels for 11% -> 0%
where the time goes in v4:
time: 621 us; the launch traced here: 612 us
  waiting for transfers between devices  206 us (33%)
  matrix products  177 us (29%)
  Pallas kernels  109 us (18%)
  other arithmetic  48.4 us (8%)
  starting transfers between devices  45 us (7%)
  local copies, waits for them, and re-layouts  22.4 us (4%)
    ppermute x31, waiting for transfers between devices, send(): return lax.ppermute(value, AXES, link(src_stage, dst_stage, cross))  190 us
    dot_general x4, matrix products, contract(): lax.dot_general(lhs, rhs, (((lhs_dim,), (rhs_dim,)), ((), ())), preferred...  123 us
    pallas_call x3, Pallas kernels, head_rows(): pl.pallas_call(head_kernel, out_shape=jax.ShapeDtypeStruct(table.shape, t...  73.5 us
    ppermute x31, starting transfers between devices, send(): return lax.ppermute(value, AXES, link(src_stage, dst_stage, cross))  41.6 us
    dot_general x4, matrix products, device_fn(): jnp.dot(x_act[c], w_one, preferred_element_type=jnp.float32)  33.9 us
    pallas_call x1, Pallas kernels, backward_stage(): pl.pallas_call(backward_kernel, out_shape=[jax.ShapeDtypeStruct((rows, mo...  20.2 us
    dot_general x4, matrix products, device_fn(): jnp.dot(gate_act[c], w_two, preferred_element_type=jnp.float32)  20 us
    pallas_call x1, Pallas kernels, add_rows(): pl.pallas_call(add_kernel, out_shape=jax.ShapeDtypeStruct(table.shape, ta...  15 us
  transfers between devices with their start and end apart: 34, of which 9 were waited for; matrix products, arithmetic and copies ran while one was open for 6% of the time, Pallas kernels for 0%

profile of v4, /device:TPU:0, one launch (start us, length us, event | category | flops | bytes accessed | tf_op | source)
XLA Modules:
  0.0 612.5 jit_solution(4553256007919011899)
XLA Ops:
  3.3 7.8 %gather_fusion = bf16[256,2048]{1,0:T(8,128)(2,1)S(1)} fusion(bf16[25136,2048]{1,0:T(8,128)(2,1)} %param.15, s32[1024]{0:T(1024)S(1)} %pad_clamp_fusion), kind=kCustom, calls=%fused_computation | custom fusion | bytes 2098176 | tf_op jit(solution)/shard_map/jit(_take)/gather | solution.py:180
  11.3 5.3 collective-permute-start
  16.6 12.8 %collective-permute-done = bf16[256,2048]{1,0:T(8,128)(2,1)S(1)} collective-permute-done((bf16[256,2048]{1,0:T(8,128)(2,1)S(1)}, bf16[256,2048]{1,0:T(8,128)(2,1)S(1)}, u32[]{:S(2)}, u32[]{:S(2)}) %collective-permute-start) | collective-permute-done | bytes 1048608 | tf_op jit(solution)/shard_map/ppermute | solution.py:137
  29.7 8.3 %fusion.72 = f32[256,4096]{1,0:T(8,128)S(1)} fusion(bf16[256,2048]{1,0:T(8,128)(2,1)S(1)} %fusion.104, bf16[1,2048,4096]{2,1,0:T(8,128)(2,1)} %param.16), kind=kOutput, calls=%fused_computation.163 | convolution fusion | flops 4294967296 | bytes 22020096 | tf_op jit(solution)/shard_map/dot_general | solution.py:187
  40.1 5.0 fusion.43
  50.4 12.8 %collective-permute-done.1 = f32[128,2048]{1,0:T(8,128)S(1)} collective-permute-done((f32[128,2048]{1,0:T(8,128)S(1)}, f32[128,2048]{1,0:T(8,128)S(1)}, u32[]{:S(2)}, u32[]{:S(2)}) %collective-permute-start.1) | collective-permute-done | bytes 1048608 | tf_op jit(solution)/shard_map/ppermute | solution.py:137
  68.3 6.4 %collective-permute-done.3 = bf16[128,2048]{1,0:T(8,128)(2,1)S(1)} collective-permute-done((bf16[128,2048]{1,0:T(8,128)(2,1)}, bf16[128,2048]{1,0:T(8,128)(2,1)S(1)}, u32[]{:S(2)}, u32[]{:S(2)}) %collective-permute-start.3) | collective-permute-done | bytes 524320 | tf_op jit(solution)/shard_map/ppermute | solution.py:137
  75.2 8.4 %fusion.70 = f32[256,4096]{1,0:T(8,128)S(1)} fusion(bf16[256,2048]{1,0:T(8,128)(2,1)S(1)} %maximum_select_fusion, bf16[1,2048,4096]{2,1,0:T(8,128)(2,1)} %param.16), kind=kOutput, calls=%fused_computation.161 | convolution fusion | flops 4294967296 | bytes 22020096 | tf_op jit(solution)/shard_map/dot_general | solution.py:187
  85.5 5.0 fusion.41
  93.8 8.4 %fusion.68 = f32[256,4096]{1,0:T(8,128)S(1)} fusion(bf16[256,2048]{1,0:T(8,128)(2,1)S(1)} %maximum_select_fusion.1, bf16[1,2048,4096]{2,1,0:T(8,128)(2,1)} %param.16), kind=kOutput, calls=%fused_computation.159 | convolution fusion | flops 4294967296 | bytes 22020096 | tf_op jit(solution)/shard_map/dot_general | solution.py:187
  104.1 5.0 fusion.39
  112.5 8.8 %fusion.66 = f32[256,4096]{1,0:T(8,128)S(1)} fusion(bf16[256,2048]{1,0:T(8,128)(2,1)S(1)} %maximum_select_fusion.2, bf16[1,2048,4096]{2,1,0:T(8,128)(2,1)} %param.16), kind=kOutput, calls=%fused_computation.157 | convolution fusion | flops 4294967296 | bytes 22020096 | tf_op jit(solution)/shard_map/dot_general | solution.py:187
  123.1 5.0 fusion.61
  132.7 77.5 %collective-permute-done.13 = bf16[128,2048]{1,0:T(8,128)(2,1)S(1)} collective-permute-done((bf16[128,2048]{1,0:T(8,128)(2,1)S(1)}, bf16[128,2048]{1,0:T(8,128)(2,1)S(1)}, u32[]{:S(2)}, u32[]{:S(2)}) %collective-permute-start.13) | collective-permute-done | bytes 524320 | tf_op jit(solution)/shard_map/ppermute | solution.py:137
  212.7 13.4 %collective-permute-done.15 = bf16[128,2048]{1,0:T(8,128)(2,1)S(1)} collective-permute-done((bf16[128,2048]{1,0:T(8,128)(2,1)S(1)}, bf16[128,2048]{1,0:T(8,128)(2,1)S(1)}, u32[]{:S(2)}, u32[]{:S(2)}) %collective-permute-start.15) | collective-permute-done | bytes 524320 | tf_op jit(solution)/shard_map/ppermute | solution.py:176
  228.1 49.6 %fusion.91 = (f32[256]{0:T(256)S(1)}, f32[256,25136]{0,1:T(8,128)}) fusion(bf16[256,2048]{1,0:T(8,128)(2,1)S(1)} %get-tuple-element.250, bf16[25136,2048]{1,0:T(8,128)(2,1)} %param.15), kind=kOutput, calls=%fused_computation.179 | convolution fusion | flops 26363441152 | bytes 129745920 | tf_op jit(solution)/shard_map/dot_general | solution.py:17
  277.7 13.2 %fusion.1 = (f32[256]{0:T(256)S(1)}, f32[256]{0:T(256)S(1)}) fusion(f32[256,25136]{0,1:T(8,128)} %get-tuple-element.271, f32[256]{0:T(256)S(1)} %get-tuple-element.270, s32[256]{0:T(256)S(1)} %sub.134), kind=kLoop, calls=%fused_computation.5 | loop fusion | flops 32173568 | bytes 25743360 | tf_op jit(solution)/shard_map/reduce_sum | solution.py:204
  295.1 8.4 %fusion.5 = bf16[25136,256]{1,0:T(8,128)(2,1)} fusion(f32[256,25136]{0,1:T(8,128)S(1)} %copy-done.1, f32[256]{0:T(256)S(1)} %bitcast.79, s32[256]{0:T(256)S(1)} %sub.134), kind=kLoop, calls=%fused_computation.9 | loop fusion | flops 32174080 | bytes 38610944 | tf_op jit(solution)/shard_map/convert_element_type | solution.py:210
  303.5 40.9 %fusion.92 = f32[256,2048]{1,0:T(8,128)S(1)} fusion(bf16[25136,256]{1,0:T(8,128)(2,1)} %fusion.5, bf16[25136,2048]{1,0:T(8,128)(2,1)} %param.15), kind=kOutput, calls=%fused_computation.180 | convolution fusion | flops 26357006336 | bytes 117923840 | tf_op jit(solution)/shard_map/dot_general | solution.py:17
  351.2 26.7 %conditional.4 = (f32[256,2048]{1,0:T(8,128)S(1)}, bf16[256,4096]{1,0:T(8,128)(2,1)}, f32[25136,2048]{1,0:T(8,128)}) conditional(s32[]{:T(128)} %convert_element_type.113, (s32[]{:T(128)}, bf16[25136,256]{1,0:T(8,128)(2,1)}, bf16[256,2048]{1,0:T(8,128)(2,1)S(1)}, f32[25136,2048]{1,0:T(8,128)}) %tuple.49, (bf16[256,2048]{1,0:T(8,128)(2,1)}, ...), branch_computations={%region_6.7_spmd, %region_7.8_spmd} | conditional | flops 8858370048 | bytes 73400392 | solution.py:238
  351.4 24.7 %head_rows.8 = f32[25136,2048]{1,0:T(8,128)} custom-call(s32[1]{0:T(128)} %bitcast.base_ref, bf16[25136,256]{1,0:T(8,128)(2,1)} %get-tuple-element.159.grad_ref, bf16[256,2048]{1,0:T(8,128)(2,1)S(1)} %get-tuple-element.160.normed_ref, f32[25136,2048]{1,0:T(8,128)} %get-tuple-element.161.table_in), custom_call_target="tpu_custom_call", output_to_operand_aliasing={{}: (3, {})} | custom-call | flops 8858370048 | bytes 69206016 | tf_op jit(solution)/shard_map/cond/branch_0_fun/head_rows/pallas_call | solution.py:31
  383.9 25.0 %conditional.5 = (f32[256,2048]{1,0:T(8,128)S(1)}, bf16[256,4096]{1,0:T(8,128)(2,1)}, f32[25136,2048]{1,0:T(8,128)}) conditional(s32[]{:T(128)} %convert_element_type.112, (s32[]{:T(128)}, bf16[25136,256]{1,0:T(8,128)(2,1)}, bf16[256,2048]{1,0:T(8,128)(2,1)S(1)}, f32[25136,2048]{1,0:T(8,128)}, bf16[256,4096]{1,0:T(8,128)(2,1)}) %tuple.51, ...), branch_computations={%region_8.9_spmd, %region_9.10_spmd} | conditional | flops 8858370048 | bytes 71303240 | solution.py:238
  383.9 24.7 %head_rows.9 = f32[25136,2048]{1,0:T(8,128)} custom-call(s32[1]{0:T(128)} %bitcast.1.base_ref, bf16[25136,256]{1,0:T(8,128)(2,1)} %get-tuple-element.171.grad_ref, bf16[256,2048]{1,0:T(8,128)(2,1)S(1)} %get-tuple-element.172.normed_ref, f32[25136,2048]{1,0:T(8,128)} %get-tuple-element.173.table_in), custom_call_target="tpu_custom_call", output_to_operand_aliasing={{}: (3, {})} | custom-call | flops 8858370048 | bytes 69206016 | tf_op jit(solution)/shard_map/cond/branch_0_fun/head_rows/pallas_call | solution.py:31
  412.6 24.4 %conditional.6 = (f32[256,2048]{1,0:T(8,128)S(1)}, bf16[256,4096]{1,0:T(8,128)(2,1)}, f32[25136,2048]{1,0:T(8,128)}) conditional(s32[]{:T(128)} %convert_element_type.111, (s32[]{:T(128)}, bf16[25136,256]{1,0:T(8,128)(2,1)}, bf16[256,2048]{1,0:T(8,128)(2,1)S(1)}, f32[25136,2048]{1,0:T(8,128)}, bf16[256,4096]{1,0:T(8,128)(2,1)}) %tuple.53, ...), branch_computations={%region_10.11_spmd, %region_11.12_spmd} | conditional | flops 8858370048 | bytes 71303240 | solution.py:238
  412.6 24.1 %head_rows.10 = f32[25136,2048]{1,0:T(8,128)} custom-call(s32[1]{0:T(128)} %bitcast.2.base_ref, bf16[25136,256]{1,0:T(8,128)(2,1)} %get-tuple-element.183.grad_ref, bf16[256,2048]{1,0:T(8,128)(2,1)S(1)} %get-tuple-element.184.normed_ref, f32[25136,2048]{1,0:T(8,128)} %get-tuple-element.185.table_in), custom_call_target="tpu_custom_call", output_to_operand_aliasing={{}: (3, {})} | custom-call | flops 8858370048 | bytes 69206016 | tf_op jit(solution)/shard_map/cond/branch_0_fun/head_rows/pallas_call | solution.py:31
  441.4 70.0 %collective-permute-done.26 = bf16[128,2048]{1,0:T(8,128)(2,1)S(1)} collective-permute-done((bf16[128,2048]{1,0:T(8,128)(2,1)}, bf16[128,2048]{1,0:T(8,128)(2,1)S(1)}, u32[]{:S(2)}, u32[]{:S(2)}) %collective-permute-start.26) | collective-permute-done | bytes 524320 | tf_op jit(solution)/shard_map/ppermute | solution.py:137
  511.4 6.7 %collective-permute-done.27 = bf16[128,2048]{1,0:T(8,128)(2,1)S(1)} collective-permute-done((bf16[128,2048]{1,0:T(8,128)(2,1)}, bf16[128,2048]{1,0:T(8,128)(2,1)S(1)}, u32[]{:S(2)}, u32[]{:S(2)}) %collective-permute-start.27) | collective-permute-done | bytes 524320 | tf_op jit(solution)/shard_map/ppermute | solution.py:137
  518.6 20.5 %conditional.7 = (f32[256,2048]{1,0:T(8,128)S(1)}, bf16[256,4096]{1,0:T(8,128)(2,1)}, f32[25136,2048]{1,0:T(8,128)}) conditional(s32[]{:T(128)} %convert_element_type.108, (s32[]{:T(128)}, bf16[25136,256]{1,0:T(8,128)(2,1)}, bf16[256,2048]{1,0:T(8,128)(2,1)S(1)}, f32[25136,2048]{1,0:T(8,128)}, bf16[256,4096]{1,0:T(8,128)(2,1)}) %tuple.55, ...), branch_computations={%region_12.13_spmd, %region_13.14_spmd} | conditional | flops 8858370048 | bytes 71303240 | solution.py:238
  518.9 20.2 %backward_stage.7 = (f32[256,2048]{1,0:T(8,128)S(1)}, bf16[256,4096]{1,0:T(8,128)(2,1)}) custom-call(bf16[256,2048]{1,0:T(8,128)(2,1)S(1)} %get-tuple-element.198.dy_ref, f32[256,4096]{1,0:T(8,128)} %get-tuple-element.199.hidden_ref, bf16[2048,4096]{1,0:T(8,128)(2,1)} %get-tuple-element.200.w_one_ref, bf16[4096,2048]{1,0:T(8,128)(2,1)} %get-tuple-element.201.w_two_ref), custom_call_target="tpu_custom_call" | custom-call | flops 8589934592 | bytes 33554432 | tf_op jit(solution)/shard_map/cond/branch_1_fun/backward_stage/pallas_call | solution.py:117
  544.3 16.7 %fusion.87 = f32[4096,2048]{1,0:T(8,128)} fusion(bf16[256,2048]{1,0:T(8,128)(2,1)S(1)} %maximum_select_fusion.5, f32[256,4096]{1,0:T(8,128)} %copy-done), kind=kOutput, calls=%fused_computation.178 | convolution fusion | flops 4304404480 | bytes 38797312 | tf_op jit(solution)/shard_map/dot_general | solution.py:17
  578.8 15.7 %convolution_bitcast_fusion = f32[1,2048,4096]{2,1,0:T(8,128)} fusion(bf16[256,2048]{1,0:T(8,128)(2,1)S(1)} %copy-done.8, bf16[256,4096]{1,0:T(8,128)(2,1)} %get-tuple-element.232), kind=kOutput, calls=%fused_computation.11 | convolution fusion | flops 4294967296 | bytes 36700160 | tf_op jit(solution)/shard_map/dot_general | solution.py:17
  595.8 15.0 %add_rows.1 = f32[25136,2048]{1,0:T(8,128)} custom-call(s32[256]{0:T(256)S(1)} %broadcast_maximum_fusion.group_ref, s32[256]{0:T(256)S(1)} %get-tuple-element.240.used_ref, bf16[2048,256]{1,0:T(8,128)(2,1)S(1)} %and_convert_fusion.pick_ref, bf16[256,2048]{1,0:T(8,128)(2,1)S(1)} %pad_maximum_fusion.2.rows_ref, ...), custom_call_target="tpu_custom_call", output_to_operand_aliasing={{}: (4, {})} | custom-call | tf_op jit(solution)/shard_map/add_rows/pallas_call | solution.py:85
  (215 shorter events, 88.1 us)
Async XLA Ops:
  11.3 18.1 %collective-permute-start = (bf16[256,2048]{1,0:T(8,128)(2,1)S(1)}, bf16[256,2048]{1,0:T(8,128)(2,1)S(1)}, u32[]{:S(2)}, u32[]{:S(2)}) collective-permute-start(bf16[256,2048]{1,0:T(8,128)(2,1)S(1)} %select_select_fusion), channel_id=1, source_target_pairs={{0,4},{4,0}} | collective-permute-start | bytes 3145736 | tf_op jit(solution)/shard_map/ppermute | solution.py:137
  46.5 16.7 %collective-permute-start.1 = (f32[128,2048]{1,0:T(8,128)S(1)}, f32[128,2048]{1,0:T(8,128)S(1)}, u32[]{:S(2)}, u32[]{:S(2)}) collective-permute-start(f32[128,2048]{1,0:T(8,128)S(1)} %constant_dynamic-slice_fusion.8), channel_id=1, source_target_pairs={{0,4},{4,0}} | collective-permute-start | bytes 3145736 | tf_op jit(solution)/shard_map/ppermute | solution.py:137
  65.4 2.9 collective-permute-start.2
  66.8 8.0 %collective-permute-start.3 = (bf16[128,2048]{1,0:T(8,128)(2,1)}, bf16[128,2048]{1,0:T(8,128)(2,1)S(1)}, u32[]{:S(2)}, u32[]{:S(2)}) collective-permute-start(bf16[128,2048]{1,0:T(8,128)(2,1)} %add_convert_fusion.7), channel_id=1, source_target_pairs={{0,5},{4,1}} | collective-permute-start | bytes 1572872 | tf_op jit(solution)/shard_map/ppermute | solution.py:137
  90.6 0.7 collective-permute-start.4
  91.6 1.7 collective-permute-start.5
  92.3 1.0 collective-permute-start.6
  109.2 0.7 collective-permute-start.7
  110.1 1.9 collective-permute-start.8
  110.8 1.2 collective-permute-start.9
  128.3 0.7 collective-permute-start.10
  129.2 1.4 collective-permute-start.12
  129.9 2.7 collective-permute-start.11
  130.6 79.5 %collective-permute-start.13 = (bf16[128,2048]{1,0:T(8,128)(2,1)S(1)}, bf16[128,2048]{1,0:T(8,128)(2,1)S(1)}, u32[]{:S(2)}, u32[]{:S(2)}) collective-permute-start(bf16[128,2048]{1,0:T(8,128)(2,1)S(1)} %collective-permute-done.12), channel_id=1, source_target_pairs={{1,0},{5,4}} | collective-permute-start | bytes 1572872 | tf_op jit(solution)/shard_map/ppermute | solution.py:137
  131.9 80.8 %collective-permute-start.14 = (bf16[128,2048]{1,0:T(8,128)(2,1)S(1)}, bf16[128,2048]{1,0:T(8,128)(2,1)S(1)}, u32[]{:S(2)}, u32[]{:S(2)}) collective-permute-start(bf16[128,2048]{1,0:T(8,128)(2,1)S(1)} %add_convert_fusion.4), channel_id=1, source_target_pairs={{3,7},{7,3}} | collective-permute-start | bytes 1572872 | tf_op jit(solution)/shard_map/ppermute | solution.py:137
  210.2 15.9 %collective-permute-start.15 = (bf16[128,2048]{1,0:T(8,128)(2,1)S(1)}, bf16[128,2048]{1,0:T(8,128)(2,1)S(1)}, u32[]{:S(2)}, u32[]{:S(2)}) collective-permute-start(bf16[128,2048]{1,0:T(8,128)(2,1)S(1)} %add_add_fusion.1), channel_id=1, source_target_pairs={{0,4},{4,0},{1,5},{5,1},{2,6},{6,2}} | collective-permute-start | bytes 1572872 | tf_op jit(solution)/shard_map/ppermute | solution.py:176
  290.9 3.6 collective-permute-start.16
  344.5 0.9 collective-permute-start.17
  378.0 0.7 collective-permute-start.19
  380.9 1.4 collective-permute-start.20
  381.6 0.7 collective-permute-start.21
  409.0 0.7 collective-permute-start.22
  410.7 1.4 collective-permute-start.23
  437.1 0.7 collective-permute-start.25
  438.8 72.6 %collective-permute-start.26 = (bf16[128,2048]{1,0:T(8,128)(2,1)}, bf16[128,2048]{1,0:T(8,128)(2,1)S(1)}, u32[]{:S(2)}, u32[]{:S(2)}) collective-permute-start(bf16[128,2048]{1,0:T(8,128)(2,1)} %add_convert_fusion.1), channel_id=1, source_target_pairs={{1,0},{5,4}} | collective-permute-start | bytes 1572872 | tf_op jit(solution)/shard_map/ppermute | solution.py:137
  440.1 78.0 %collective-permute-start.27 = (bf16[128,2048]{1,0:T(8,128)(2,1)}, bf16[128,2048]{1,0:T(8,128)(2,1)S(1)}, u32[]{:S(2)}, u32[]{:S(2)}) collective-permute-start(bf16[128,2048]{1,0:T(8,128)(2,1)} %add_convert_fusion.1), channel_id=1, source_target_pairs={{1,4},{5,0}} | collective-permute-start | bytes 1572872 | tf_op jit(solution)/shard_map/ppermute | solution.py:137
  540.6 20.6 %collective-permute-start.28 = (f32[128,2048]{1,0:T(8,128)S(1)}, f32[128,2048]{1,0:T(8,128)S(1)}, u32[]{:S(2)}, u32[]{:S(2)}) collective-permute-start(f32[128,2048]{1,0:T(8,128)S(1)} %constant_dynamic-slice_fusion), channel_id=1, source_target_pairs={{0,4},{4,0}} | collective-permute-start | bytes 3145736 | tf_op jit(solution)/shard_map/ppermute | solution.py:137
  562.2 7.9 %collective-permute-start.30 = (bf16[128,2048]{1,0:T(8,128)(2,1)}, bf16[128,2048]{1,0:T(8,128)(2,1)S(1)}, u32[]{:S(2)}, u32[]{:S(2)}) collective-permute-start(bf16[128,2048]{1,0:T(8,128)(2,1)} %add_convert_fusion), channel_id=1, source_target_pairs={{0,2},{4,6}} | collective-permute-start | bytes 1572872 | tf_op jit(solution)/shard_map/ppermute | solution.py:137
  564.0 12.6 %collective-permute-start.29 = (bf16[128,2048]{1,0:T(8,128)(2,1)}, bf16[128,2048]{1,0:T(8,128)(2,1)}, u32[]{:S(2)}, u32[]{:S(2)}) collective-permute-start(bf16[128,2048]{1,0:T(8,128)(2,1)} %add_convert_fusion), channel_id=1, source_target_pairs={{0,1},{4,5}} | collective-permute-start | bytes 1572872 | tf_op jit(solution)/shard_map/ppermute | solution.py:137
  570.1 6.5 %collective-permute-start.31 = (bf16[128,2048]{1,0:T(8,128)(2,1)S(1)}, bf16[128,2048]{1,0:T(8,128)(2,1)}, u32[]{:S(2)}, u32[]{:S(2)}) collective-permute-start(bf16[128,2048]{1,0:T(8,128)(2,1)S(1)} %collective-permute-done.30), channel_id=1, source_target_pairs={{2,3},{6,7}} | collective-permute-start | bytes 1572872 | tf_op jit(solution)/shard_map/ppermute | solution.py:137
  574.4 20.1 %collective-permute-start.32 = (bf16[128,2048]{1,0:T(8,128)(2,1)}, bf16[128,2048]{1,0:T(8,128)(2,1)S(1)}, u32[]{:S(2)}, u32[]{:S(2)}) collective-permute-start(bf16[128,2048]{1,0:T(8,128)(2,1)} %add_convert_fusion), channel_id=1, source_target_pairs={{0,4},{4,0}} | collective-permute-start | bytes 1572872 | tf_op jit(solution)/shard_map/ppermute | solution.py:137
  578.1 16.4 %collective-permute-start.33 = (bf16[128,2048]{1,0:T(8,128)(2,1)S(1)}, bf16[128,2048]{1,0:T(8,128)(2,1)S(1)}, u32[]{:S(2)}, u32[]{:S(2)}) collective-permute-start(bf16[128,2048]{1,0:T(8,128)(2,1)S(1)} %add_add_fusion), channel_id=1, source_target_pairs={{1,5},{5,1},{2,6},{6,2},{3,7},{7,3}} | collective-permute-start | bytes 1572872 | tf_op jit(solution)/shard_map/ppermute | solution.py:176
  (42 other events, 403.0 us)
